TPU v7x, 256 devices: a 8x8x2 block of a 8x8x16 slice. The times are simulated.
256 devices in a mesh: parts: 2 (over z), uly: 8 (over x), blk: 16 (over y, core).
Axes of the slice: x: 8, y: 8, z: 2, core: 2. Of those that a mesh axis runs over, the one named last changes fastest.
The devices are a block of a 8x8x16 slice.
Arguments:
- queries: bfloat16 [32, 512, 8192], P(('parts', 'blk'), 'uly'), parts along dimension 0, may hold values from -4.5 to 4.5
- keys: bfloat16 [32, 512, 1024], P(('parts', 'blk'), 'uly'), parts along dimension 0, may hold values from -4.5 to 4.5
- values: bfloat16 [32, 512, 1024], P(('parts', 'blk'), 'uly'), parts along dimension 0, may hold values from -6 to 6
- doc_blocks: int32 [32], P('parts'), parts along dimension 0, may hold values from 1 to 36, 64 in all
Outputs:
- attended: bfloat16 [32, 512, 8192], P(('parts', 'blk'), 'uly'), parts along dimension 0
There are 2 independent parts, one for each index of `parts`. A program takes and returns all parts, laid end to end along the dimension named above; each array names one. Nothing has to cross between parts.
Inputs may be any that keep to these rules, and one draw needn't show every extreme that they name: `doc_blocks`: the lengths sum to 64; the longest document holds exactly (9) * 512 tokens.
All inputs are finite; a program needn't handle non-finite values.
Results may differ from a plain program's by a relative error of at most 0.0037.
Values may be sent and summed in bfloat16 or wider, within the bound.
No kernel may reach another device: no remote copies, remote signals or barrier semaphores. Data moves between devices by JAX's collectives and lax.ppermute only.
A program may use at most 128 MiB of HBM per device.

v0:
```python
import jax
import jax.numpy as jnp
from jax import lax
from jax.sharding import PartitionSpec as P

HEAD_WIDTH = 128
BLOCK = 128


def side_by_side(arrays, axis, split_dim, concat_dim, along):
    ends, at = ([], 0)
    for a in arrays[:-1]:
        at += a.shape[along]
        ends.append(at)
    both = jnp.concatenate(arrays, axis=along)
    return tuple(
        jnp.split(
            lax.all_to_all(both, axis, split_axis=split_dim, concat_axis=concat_dim, tiled=True),
            ends,
            axis=along,
        )
    )


def segment_of(positions, ends):
    return jnp.sum((positions[:, None] >= ends[None, :]).astype(jnp.int32), axis=1)


def on_device(queries, keys, values, doc_blocks):
    moved_q, moved_k, moved_v = (
        lax.all_to_all(queries, "uly", split_axis=2, concat_axis=1, tiled=True),
        *side_by_side((keys, values), "uly", 2, 1, 0),
    )
    slot = moved_q.shape[1]
    local_q = moved_q.shape[2] // HEAD_WIDTH
    local_kv = moved_k.shape[2] // HEAD_WIDTH
    query_group = local_q // local_kv
    scale = HEAD_WIDTH ** (-0.5)
    first_index = lax.axis_index("blk") * slot
    ends = jnp.cumsum(doc_blocks) * BLOCK
    qpos = first_index + jnp.arange(slot, dtype=jnp.int32)
    qseg = segment_of(qpos, ends)
    qheads = jnp.transpose(moved_q[0].reshape(slot, local_q, HEAD_WIDTH), (1, 0, 2))
    stacked = jnp.concatenate([moved_k, moved_v], axis=0)

    def allowed_for(kpos):
        kseg = segment_of(kpos, ends)
        return (qseg[:, None] == kseg[None, :]) & (kpos[None, :] <= qpos[:, None])

    start_state = (
        jnp.full((local_q, slot), -1e30, jnp.float32),
        jnp.zeros((local_q, slot), jnp.float32),
        jnp.zeros((local_q, slot, HEAD_WIDTH), jnp.float32),
    )
    piece = lax.all_gather(stacked, "blk", axis=1, tiled=True)
    start = jnp.int32(0)
    count = piece.shape[1]

    def work(state):
        key_piece = piece[0].reshape(count, local_kv, HEAD_WIDTH)
        value_piece = piece[1].reshape(count, local_kv, HEAD_WIDTH)
        allowed = allowed_for(jnp.arange(count, dtype=jnp.int32))

        def one_head(inputs):
            head, running, summed, accum = inputs
            qh = lax.dynamic_index_in_dim(qheads, head, 0, keepdims=False)
            kh = lax.dynamic_index_in_dim(key_piece, head // query_group, 1, keepdims=False)
            vh = lax.dynamic_index_in_dim(value_piece, head // query_group, 1, keepdims=False)
            scores = jnp.dot(qh, kh.T, preferred_element_type=jnp.float32) * scale
            scores = jnp.where(allowed, scores, -1e30)
            newest = jnp.maximum(running, jnp.max(scores, axis=1))
            expo = jnp.where(allowed, jnp.exp(scores - newest[:, None]), 0.0)
            factor = jnp.exp(running - newest)
            summed = summed * factor + jnp.sum(expo, axis=1)
            accum = accum * factor[:, None] + jnp.dot(
                expo.astype(jnp.bfloat16), vh, preferred_element_type=jnp.float32
            )
            return (newest, summed, accum)

        return lax.map(one_head, (jnp.arange(local_q, dtype=jnp.int32),) + tuple(state))

    last_seg = jnp.sum((start + count - 1 >= ends).astype(jnp.int32))
    useful = (start < first_index + slot) & (last_seg >= qseg[0])
    running, summed, accum = lax.cond(useful, work, lambda state: state, start_state)
    heads = (accum / summed[:, :, None]).astype(jnp.bfloat16)
    outputs = jnp.transpose(heads, (1, 0, 2)).reshape(1, slot, local_q * HEAD_WIDTH)
    return lax.all_to_all(outputs, "uly", split_axis=1, concat_axis=2, tiled=True)


def solution(mesh):
    return jax.shard_map(
        on_device,
        mesh=mesh,
        in_specs=(
            P(("parts", "blk"), "uly", None),
            P(("parts", "blk"), "uly", None),
            P(("parts", "blk"), "uly", None),
            P("parts"),
        ),
        out_specs=P(("parts", "blk"), "uly", None),
        check_vma=False,
    )
```

profile of v0, /device:TPU:720, one launch (start us, length us, event | category | flops | bytes accessed | tf_op | source)
XLA Modules:
  0.0 406.6 jit_solution(11912159211561026626)
XLA Ops:
  8.3 19.1 %all_to_all.48 = bf16[8,2,8192]{2,1,0:T(2,128)(2,1)S(1)} all-to-all(bf16[8,2,8192]{2,1,0:T(2,128)(2,1)S(1)} %reshape.78), channel_id=1, replica_groups=mesh['parts'=2,'uly'=8,'blk'=16] {'uly'}, dimensions={0} | all-to-all | bytes 524288 | tf_op jit(solution)/shard_map/all_to_all | solution.py:18
  30.2 9.2 %copy.58 = bf16[1,64,8192]{1,0,2:T(2,128)(2,1)} copy(bf16[1,64,8192]{2,1,0:T(8,128)(2,1)} %param.8) | data formatting | bytes 2097152 | tf_op args[0]
  39.9 45.1 %reduce.2 = bf16[8192,64]{1,0:T(8,128)(2,1)S(1)} reduce(bf16[8192,1,64]{2,1,0:T(2,128)(2,1)} %bitcast.72, bf16[]{:T(256)} %broadcast.102), dimensions={1}, to_apply=%bitcast.51.reduce_sub_computation | reduce | bytes 2097154
  85.0 2.7 reshape.80
  87.6 3.8 all-to-all-start.1
  94.2 24.5 %all-to-all-done.1 = bf16[8,2,32768]{2,1,0:T(2,128)(2,1)S(1)} async-done(((bf16[8,2,32768]{2,1,0:T(2,128)(2,1)}), bf16[8,2,32768]{2,1,0:T(2,128)(2,1)S(1)}, u32[]{:S(2)}, u32[]{:S(2)}) %all-to-all-start.1) | async-done | bytes 1048608 | tf_op jit(solution)/shard_map/all_to_all | solution.py:31
  118.7 4.3 %reshape.81 = bf16[8192,1,64]{2,1,0:T(2,128)(2,1)} reshape(bf16[8,2,32768]{2,1,0:T(2,128)(2,1)S(1)} %all-to-all-done.1) | data formatting | bytes 2097152
  123.1 8.2 %copy.59 = bf16[1,64,8192]{2,1,0:T(8,128)(2,1)S(1)} copy(bf16[1,64,8192]{1,0,2:T(2,128)(2,1)} %bitcast.73) | data formatting | bytes 2097152 | tf_op jit(solution)/shard_map/all_to_all | solution.py:31
  132.8 221.4 %conditional.1 = (f32[8,512]{1,0:T(8,128)}, f32[8,512,128]{1,2,0:T(8,128)}) conditional(s32[]{:T(128)} %convert_element_type.20, () %tuple.17, (bf16[2,8192,128]{2,1,0:T(8,128)(2,1)}, s32[512]{0:T(512)S(1)}, s32[16]{0:T(128)S(1)}, s32[]{:T(128)}, s32[512]{0:T(512)S(1)}, /*index=5*/bf16[8,512,128]{2,0,1:T(8,128)(2,1)S(1)}) %tuple.53), branch_computations={%region_3.4_spmd, %region_4.10_spmd} | conditional | flops 2240210944 | bytes 133736896 | solution.py:84
  133.0 1.1 copy.61
  134.2 3.8 slice_bitcast_fusion
  138.2 216.0 %while.12 = (s32[]{:T(128)}, f32[8,512]{1,0:T(8,128)}, f32[8,512,128]{1,2,0:T(8,128)}, s32[8]{0:T(128)S(1)}, bf16[8,512,128]{2,1,0:T(8,128)(2,1)}, /*index=5*/bf...) while((s32[]{:T(128)}, f32[8,512]{1,0:T(8,128)}, ...), condition=%wide.region_9.9_spmd.clone, body=%wide.region_6.8_spmd.clone.sunk | while | flops 2239825408 | bytes 123214048 | solution.py:80
  141.0 6.8 %fusion.37 = (f32[512]{0:T(512)S(1)}, f32[512,8192]{1,0:T(8,128)S(1)}) fusion(s32[512]{0:T(512)S(1)} %get-tuple-element.266, s32[8192]{0:T(1024)S(1)} %get-tuple-element.264, s32[512]{0:T(512)S(1)} %get-tuple-element.265, bf16[8192,1,128]{2,0,1:T(8,128)(2,1)} %get-tuple-element.262, bf16[8,512,128]{2,1,0:T(8,128)(2,1)} %get-tuple-element.261, ...), kind=kOutput, calls=%fused_computation.5.clone.1 | convolution fusion | flops 1098907136 | bytes 19044356 | tf_op jit(solution)/shard_map/cond/branch_1_fun/while/body/eval_jaxpr/dot_general | solution.py:69
  147.8 6.2 %fusion.38 = f32[512]{0:T(512)S(1)} fusion(f32[512,8192]{1,0:T(8,128)S(1)} %get-tuple-element.228, s32[512]{0:T(512)S(1)} %get-tuple-element.266, s32[8192]{0:T(1024)S(1)} %get-tuple-element.264, f32[512]{0:T(512)S(1)} %broadcast_maximum_fusion.2, s32[512]{0:T(512)S(1)} %get-tuple-element.265), kind=kLoop, calls=%fused_computation.7.clone.1 | loop fusion | flops 33553920 | bytes 16818176 | tf_op jit(solution)/shard_map/cond/branch_1_fun/while/body/eval_jaxpr/reduce_sum | solution.py:74
  153.9 1.3 dynamic_update_slice.14
  155.3 9.1 %fusion.39 = f32[1,512,128]{2,1,0:T(8,128)S(1)} fusion(bf16[8192,1,128]{2,0,1:T(8,128)(2,1)S(1)} %get-tuple-element.263, f32[512,8192]{1,0:T(8,128)} %copy-done, s32[512]{0:T(512)S(1)} %get-tuple-element.266, s32[8192]{0:T(1024)S(1)} %get-tuple-element.264, f32[512]{0:T(512)S(1)} %broadcast_maximum_fusion.2, s32[512]{0:T(512)S(1)} %get-tuple-element.265, ...), kind=kOutput, calls=%fused_computation.13.clone.1 | convolution fusion | flops 1107361792 | bytes 19177472 | tf_op jit(solution)/shard_map/cond/branch_1_fun/while/body/eval_jaxpr/dot_general | solution.py:75
  168.0 6.8 %fusion.37 = (f32[512]{0:T(512)S(1)}, f32[512,8192]{1,0:T(8,128)S(1)}) fusion(s32[512]{0:T(512)S(1)} %get-tuple-element.266, s32[8192]{0:T(1024)S(1)} %get-tuple-element.264, s32[512]{0:T(512)S(1)} %get-tuple-element.265, bf16[8192,1,128]{2,0,1:T(8,128)(2,1)} %get-tuple-element.262, bf16[8,512,128]{2,1,0:T(8,128)(2,1)} %get-tuple-element.261, ...), kind=kOutput, calls=%fused_computation.5.clone.1 | convolution fusion | flops 1098907136 | bytes 19044356 | tf_op jit(solution)/shard_map/cond/branch_1_fun/while/body/eval_jaxpr/dot_general | solution.py:69
  174.8 6.2 %fusion.38 = f32[512]{0:T(512)S(1)} fusion(f32[512,8192]{1,0:T(8,128)S(1)} %get-tuple-element.228, s32[512]{0:T(512)S(1)} %get-tuple-element.266, s32[8192]{0:T(1024)S(1)} %get-tuple-element.264, f32[512]{0:T(512)S(1)} %broadcast_maximum_fusion.2, s32[512]{0:T(512)S(1)} %get-tuple-element.265), kind=kLoop, calls=%fused_computation.7.clone.1 | loop fusion | flops 33553920 | bytes 16818176 | tf_op jit(solution)/shard_map/cond/branch_1_fun/while/body/eval_jaxpr/reduce_sum | solution.py:74
  180.9 1.3 dynamic_update_slice.14
  182.3 9.1 %fusion.39 = f32[1,512,128]{2,1,0:T(8,128)S(1)} fusion(bf16[8192,1,128]{2,0,1:T(8,128)(2,1)S(1)} %get-tuple-element.263, f32[512,8192]{1,0:T(8,128)} %copy-done, s32[512]{0:T(512)S(1)} %get-tuple-element.266, s32[8192]{0:T(1024)S(1)} %get-tuple-element.264, f32[512]{0:T(512)S(1)} %broadcast_maximum_fusion.2, s32[512]{0:T(512)S(1)} %get-tuple-element.265, ...), kind=kOutput, calls=%fused_computation.13.clone.1 | convolution fusion | flops 1107361792 | bytes 19177472 | tf_op jit(solution)/shard_map/cond/branch_1_fun/while/body/eval_jaxpr/dot_general | solution.py:75
  194.9 6.8 %fusion.37 = (f32[512]{0:T(512)S(1)}, f32[512,8192]{1,0:T(8,128)S(1)}) fusion(s32[512]{0:T(512)S(1)} %get-tuple-element.266, s32[8192]{0:T(1024)S(1)} %get-tuple-element.264, s32[512]{0:T(512)S(1)} %get-tuple-element.265, bf16[8192,1,128]{2,0,1:T(8,128)(2,1)} %get-tuple-element.262, bf16[8,512,128]{2,1,0:T(8,128)(2,1)} %get-tuple-element.261, ...), kind=kOutput, calls=%fused_computation.5.clone.1 | convolution fusion | flops 1098907136 | bytes 19044356 | tf_op jit(solution)/shard_map/cond/branch_1_fun/while/body/eval_jaxpr/dot_general | solution.py:69
  201.8 6.2 %fusion.38 = f32[512]{0:T(512)S(1)} fusion(f32[512,8192]{1,0:T(8,128)S(1)} %get-tuple-element.228, s32[512]{0:T(512)S(1)} %get-tuple-element.266, s32[8192]{0:T(1024)S(1)} %get-tuple-element.264, f32[512]{0:T(512)S(1)} %broadcast_maximum_fusion.2, s32[512]{0:T(512)S(1)} %get-tuple-element.265), kind=kLoop, calls=%fused_computation.7.clone.1 | loop fusion | flops 33553920 | bytes 16818176 | tf_op jit(solution)/shard_map/cond/branch_1_fun/while/body/eval_jaxpr/reduce_sum | solution.py:74
  208.0 1.3 dynamic_update_slice.14
  209.3 9.1 %fusion.39 = f32[1,512,128]{2,1,0:T(8,128)S(1)} fusion(bf16[8192,1,128]{2,0,1:T(8,128)(2,1)S(1)} %get-tuple-element.263, f32[512,8192]{1,0:T(8,128)} %copy-done, s32[512]{0:T(512)S(1)} %get-tuple-element.266, s32[8192]{0:T(1024)S(1)} %get-tuple-element.264, f32[512]{0:T(512)S(1)} %broadcast_maximum_fusion.2, s32[512]{0:T(512)S(1)} %get-tuple-element.265, ...), kind=kOutput, calls=%fused_computation.13.clone.1 | convolution fusion | flops 1107361792 | bytes 19177472 | tf_op jit(solution)/shard_map/cond/branch_1_fun/while/body/eval_jaxpr/dot_general | solution.py:75
  222.0 6.8 %fusion.37 = (f32[512]{0:T(512)S(1)}, f32[512,8192]{1,0:T(8,128)S(1)}) fusion(s32[512]{0:T(512)S(1)} %get-tuple-element.266, s32[8192]{0:T(1024)S(1)} %get-tuple-element.264, s32[512]{0:T(512)S(1)} %get-tuple-element.265, bf16[8192,1,128]{2,0,1:T(8,128)(2,1)} %get-tuple-element.262, bf16[8,512,128]{2,1,0:T(8,128)(2,1)} %get-tuple-element.261, ...), kind=kOutput, calls=%fused_computation.5.clone.1 | convolution fusion | flops 1098907136 | bytes 19044356 | tf_op jit(solution)/shard_map/cond/branch_1_fun/while/body/eval_jaxpr/dot_general | solution.py:69
  228.8 6.2 %fusion.38 = f32[512]{0:T(512)S(1)} fusion(f32[512,8192]{1,0:T(8,128)S(1)} %get-tuple-element.228, s32[512]{0:T(512)S(1)} %get-tuple-element.266, s32[8192]{0:T(1024)S(1)} %get-tuple-element.264, f32[512]{0:T(512)S(1)} %broadcast_maximum_fusion.2, s32[512]{0:T(512)S(1)} %get-tuple-element.265), kind=kLoop, calls=%fused_computation.7.clone.1 | loop fusion | flops 33553920 | bytes 16818176 | tf_op jit(solution)/shard_map/cond/branch_1_fun/while/body/eval_jaxpr/reduce_sum | solution.py:74
  235.0 1.3 dynamic_update_slice.14
  236.3 9.1 %fusion.39 = f32[1,512,128]{2,1,0:T(8,128)S(1)} fusion(bf16[8192,1,128]{2,0,1:T(8,128)(2,1)S(1)} %get-tuple-element.263, f32[512,8192]{1,0:T(8,128)} %copy-done, s32[512]{0:T(512)S(1)} %get-tuple-element.266, s32[8192]{0:T(1024)S(1)} %get-tuple-element.264, f32[512]{0:T(512)S(1)} %broadcast_maximum_fusion.2, s32[512]{0:T(512)S(1)} %get-tuple-element.265, ...), kind=kOutput, calls=%fused_computation.13.clone.1 | convolution fusion | flops 1107361792 | bytes 19177472 | tf_op jit(solution)/shard_map/cond/branch_1_fun/while/body/eval_jaxpr/dot_general | solution.py:75
  249.0 6.8 %fusion.37 = (f32[512]{0:T(512)S(1)}, f32[512,8192]{1,0:T(8,128)S(1)}) fusion(s32[512]{0:T(512)S(1)} %get-tuple-element.266, s32[8192]{0:T(1024)S(1)} %get-tuple-element.264, s32[512]{0:T(512)S(1)} %get-tuple-element.265, bf16[8192,1,128]{2,0,1:T(8,128)(2,1)} %get-tuple-element.262, bf16[8,512,128]{2,1,0:T(8,128)(2,1)} %get-tuple-element.261, ...), kind=kOutput, calls=%fused_computation.5.clone.1 | convolution fusion | flops 1098907136 | bytes 19044356 | tf_op jit(solution)/shard_map/cond/branch_1_fun/while/body/eval_jaxpr/dot_general | solution.py:69
  255.8 6.2 %fusion.38 = f32[512]{0:T(512)S(1)} fusion(f32[512,8192]{1,0:T(8,128)S(1)} %get-tuple-element.228, s32[512]{0:T(512)S(1)} %get-tuple-element.266, s32[8192]{0:T(1024)S(1)} %get-tuple-element.264, f32[512]{0:T(512)S(1)} %broadcast_maximum_fusion.2, s32[512]{0:T(512)S(1)} %get-tuple-element.265), kind=kLoop, calls=%fused_computation.7.clone.1 | loop fusion | flops 33553920 | bytes 16818176 | tf_op jit(solution)/shard_map/cond/branch_1_fun/while/body/eval_jaxpr/reduce_sum | solution.py:74
  262.0 1.3 dynamic_update_slice.14
  263.3 9.1 %fusion.39 = f32[1,512,128]{2,1,0:T(8,128)S(1)} fusion(bf16[8192,1,128]{2,0,1:T(8,128)(2,1)S(1)} %get-tuple-element.263, f32[512,8192]{1,0:T(8,128)} %copy-done, s32[512]{0:T(512)S(1)} %get-tuple-element.266, s32[8192]{0:T(1024)S(1)} %get-tuple-element.264, f32[512]{0:T(512)S(1)} %broadcast_maximum_fusion.2, s32[512]{0:T(512)S(1)} %get-tuple-element.265, ...), kind=kOutput, calls=%fused_computation.13.clone.1 | convolution fusion | flops 1107361792 | bytes 19177472 | tf_op jit(solution)/shard_map/cond/branch_1_fun/while/body/eval_jaxpr/dot_general | solution.py:75
  276.0 6.8 %fusion.37 = (f32[512]{0:T(512)S(1)}, f32[512,8192]{1,0:T(8,128)S(1)}) fusion(s32[512]{0:T(512)S(1)} %get-tuple-element.266, s32[8192]{0:T(1024)S(1)} %get-tuple-element.264, s32[512]{0:T(512)S(1)} %get-tuple-element.265, bf16[8192,1,128]{2,0,1:T(8,128)(2,1)} %get-tuple-element.262, bf16[8,512,128]{2,1,0:T(8,128)(2,1)} %get-tuple-element.261, ...), kind=kOutput, calls=%fused_computation.5.clone.1 | convolution fusion | flops 1098907136 | bytes 19044356 | tf_op jit(solution)/shard_map/cond/branch_1_fun/while/body/eval_jaxpr/dot_general | solution.py:69
  282.8 6.2 %fusion.38 = f32[512]{0:T(512)S(1)} fusion(f32[512,8192]{1,0:T(8,128)S(1)} %get-tuple-element.228, s32[512]{0:T(512)S(1)} %get-tuple-element.266, s32[8192]{0:T(1024)S(1)} %get-tuple-element.264, f32[512]{0:T(512)S(1)} %broadcast_maximum_fusion.2, s32[512]{0:T(512)S(1)} %get-tuple-element.265), kind=kLoop, calls=%fused_computation.7.clone.1 | loop fusion | flops 33553920 | bytes 16818176 | tf_op jit(solution)/shard_map/cond/branch_1_fun/while/body/eval_jaxpr/reduce_sum | solution.py:74
  288.9 1.3 dynamic_update_slice.14
  290.3 9.1 %fusion.39 = f32[1,512,128]{2,1,0:T(8,128)S(1)} fusion(bf16[8192,1,128]{2,0,1:T(8,128)(2,1)S(1)} %get-tuple-element.263, f32[512,8192]{1,0:T(8,128)} %copy-done, s32[512]{0:T(512)S(1)} %get-tuple-element.266, s32[8192]{0:T(1024)S(1)} %get-tuple-element.264, f32[512]{0:T(512)S(1)} %broadcast_maximum_fusion.2, s32[512]{0:T(512)S(1)} %get-tuple-element.265, ...), kind=kOutput, calls=%fused_computation.13.clone.1 | convolution fusion | flops 1107361792 | bytes 19177472 | tf_op jit(solution)/shard_map/cond/branch_1_fun/while/body/eval_jaxpr/dot_general | solution.py:75
  302.9 6.8 %fusion.37 = (f32[512]{0:T(512)S(1)}, f32[512,8192]{1,0:T(8,128)S(1)}) fusion(s32[512]{0:T(512)S(1)} %get-tuple-element.266, s32[8192]{0:T(1024)S(1)} %get-tuple-element.264, s32[512]{0:T(512)S(1)} %get-tuple-element.265, bf16[8192,1,128]{2,0,1:T(8,128)(2,1)} %get-tuple-element.262, bf16[8,512,128]{2,1,0:T(8,128)(2,1)} %get-tuple-element.261, ...), kind=kOutput, calls=%fused_computation.5.clone.1 | convolution fusion | flops 1098907136 | bytes 19044356 | tf_op jit(solution)/shard_map/cond/branch_1_fun/while/body/eval_jaxpr/dot_general | solution.py:69
  309.8 6.2 %fusion.38 = f32[512]{0:T(512)S(1)} fusion(f32[512,8192]{1,0:T(8,128)S(1)} %get-tuple-element.228, s32[512]{0:T(512)S(1)} %get-tuple-element.266, s32[8192]{0:T(1024)S(1)} %get-tuple-element.264, f32[512]{0:T(512)S(1)} %broadcast_maximum_fusion.2, s32[512]{0:T(512)S(1)} %get-tuple-element.265), kind=kLoop, calls=%fused_computation.7.clone.1 | loop fusion | flops 33553920 | bytes 16818176 | tf_op jit(solution)/shard_map/cond/branch_1_fun/while/body/eval_jaxpr/reduce_sum | solution.py:74
  316.0 1.3 dynamic_update_slice.14
  317.3 9.1 %fusion.39 = f32[1,512,128]{2,1,0:T(8,128)S(1)} fusion(bf16[8192,1,128]{2,0,1:T(8,128)(2,1)S(1)} %get-tuple-element.263, f32[512,8192]{1,0:T(8,128)} %copy-done, s32[512]{0:T(512)S(1)} %get-tuple-element.266, s32[8192]{0:T(1024)S(1)} %get-tuple-element.264, f32[512]{0:T(512)S(1)} %broadcast_maximum_fusion.2, s32[512]{0:T(512)S(1)} %get-tuple-element.265, ...), kind=kOutput, calls=%fused_computation.13.clone.1 | convolution fusion | flops 1107361792 | bytes 19177472 | tf_op jit(solution)/shard_map/cond/branch_1_fun/while/body/eval_jaxpr/dot_general | solution.py:75
  329.9 6.8 %fusion.37 = (f32[512]{0:T(512)S(1)}, f32[512,8192]{1,0:T(8,128)S(1)}) fusion(s32[512]{0:T(512)S(1)} %get-tuple-element.266, s32[8192]{0:T(1024)S(1)} %get-tuple-element.264, s32[512]{0:T(512)S(1)} %get-tuple-element.265, bf16[8192,1,128]{2,0,1:T(8,128)(2,1)} %get-tuple-element.262, bf16[8,512,128]{2,1,0:T(8,128)(2,1)} %get-tuple-element.261, ...), kind=kOutput, calls=%fused_computation.5.clone.1 | convolution fusion | flops 1098907136 | bytes 19044356 | tf_op jit(solution)/shard_map/cond/branch_1_fun/while/body/eval_jaxpr/dot_general | solution.py:69
  336.7 6.2 %fusion.38 = f32[512]{0:T(512)S(1)} fusion(f32[512,8192]{1,0:T(8,128)S(1)} %get-tuple-element.228, s32[512]{0:T(512)S(1)} %get-tuple-element.266, s32[8192]{0:T(1024)S(1)} %get-tuple-element.264, f32[512]{0:T(512)S(1)} %broadcast_maximum_fusion.2, s32[512]{0:T(512)S(1)} %get-tuple-element.265), kind=kLoop, calls=%fused_computation.7.clone.1 | loop fusion | flops 33553920 | bytes 16818176 | tf_op jit(solution)/shard_map/cond/branch_1_fun/while/body/eval_jaxpr/reduce_sum | solution.py:74
  342.9 1.3 dynamic_update_slice.14
  344.3 9.1 %fusion.39 = f32[1,512,128]{2,1,0:T(8,128)S(1)} fusion(bf16[8192,1,128]{2,0,1:T(8,128)(2,1)S(1)} %get-tuple-element.263, f32[512,8192]{1,0:T(8,128)} %copy-done, s32[512]{0:T(512)S(1)} %get-tuple-element.266, s32[8192]{0:T(1024)S(1)} %get-tuple-element.264, f32[512]{0:T(512)S(1)} %broadcast_maximum_fusion.2, s32[512]{0:T(512)S(1)} %get-tuple-element.265, ...), kind=kOutput, calls=%fused_computation.13.clone.1 | convolution fusion | flops 1107361792 | bytes 19177472 | tf_op jit(solution)/shard_map/cond/branch_1_fun/while/body/eval_jaxpr/dot_general | solution.py:75
  354.2 1.9 divide_convert_fusion
  356.1 2.0 copy.63
  358.1 6.7 %reduce.3 = bf16[512,1024]{1,0:T(8,128)(2,1)S(1)} reduce(bf16[512,1,1024]{2,1,0:T(2,128)(2,1)S(1)} %bitcast.75, bf16[]{:T(256)} %broadcast.102), dimensions={1}, to_apply=%bitcast.53.reduce_sub_computation | reduce | bytes 2097154
  365.6 31.7 %all_to_all.49 = bf16[8,2,32768]{2,1,0:T(2,128)(2,1)S(1)} all-to-all(bf16[8,2,32768]{2,1,0:T(2,128)(2,1)S(1)} %reshape.82), channel_id=1, replica_groups=mesh['parts'=2,'uly'=8,'blk'=16] {'uly'}, dimensions={0} | all-to-all | bytes 2097152 | tf_op jit(solution)/shard_map/all_to_all | solution.py:87
  (91 shorter events, 23.9 us)
Async XLA Ops:
  6.5 126.2 %all-gather.2.cloned.1.call-start = ((), (), s32[]{:S(2)}) async-start(), calls=%async_computation.3 | async-start | bytes 4456448 | tf_op jit(solution)/shard_map/all_gather | solution.py:55
  30.2 61.3 %copy-start.1 = (s32[16]{0:T(128)S(1)}, s32[16]{0:T(128)}, u32[]{:S(2)}) copy-start(s32[16]{0:T(128)} %param.11) | copy-start | bytes 196
  87.6 31.1 %all-to-all-start.1 = ((bf16[8,2,32768]{2,1,0:T(2,128)(2,1)}), bf16[8,2,32768]{2,1,0:T(2,128)(2,1)S(1)}, u32[]{:S(2)}, u32[]{:S(2)}) async-start(bf16[8,2,32768]{2,1,0:T(2,128)(2,1)} %reshape.80), calls=%async_computation.1 | async-start | bytes 2097152 | tf_op jit(solution)/shard_map/all_to_all | solution.py:31
  147.7 6.2 %copy-start = (f32[512,8192]{1,0:T(8,128)}, f32[512,8192]{1,0:T(8,128)S(1)}, u32[]{:S(2)}) copy-start(f32[512,8192]{1,0:T(8,128)S(1)} %get-tuple-element.228) | copy-start | bytes 50331652 | tf_op jit(solution)/shard_map/cond/branch_1_fun/while
  174.7 6.2 %copy-start = (f32[512,8192]{1,0:T(8,128)}, f32[512,8192]{1,0:T(8,128)S(1)}, u32[]{:S(2)}) copy-start(f32[512,8192]{1,0:T(8,128)S(1)} %get-tuple-element.228) | copy-start | bytes 50331652 | tf_op jit(solution)/shard_map/cond/branch_1_fun/while
  201.7 6.2 %copy-start = (f32[512,8192]{1,0:T(8,128)}, f32[512,8192]{1,0:T(8,128)S(1)}, u32[]{:S(2)}) copy-start(f32[512,8192]{1,0:T(8,128)S(1)} %get-tuple-element.228) | copy-start | bytes 50331652 | tf_op jit(solution)/shard_map/cond/branch_1_fun/while
  228.7 6.2 %copy-start = (f32[512,8192]{1,0:T(8,128)}, f32[512,8192]{1,0:T(8,128)S(1)}, u32[]{:S(2)}) copy-start(f32[512,8192]{1,0:T(8,128)S(1)} %get-tuple-element.228) | copy-start | bytes 50331652 | tf_op jit(solution)/shard_map/cond/branch_1_fun/while
  255.8 6.2 %copy-start = (f32[512,8192]{1,0:T(8,128)}, f32[512,8192]{1,0:T(8,128)S(1)}, u32[]{:S(2)}) copy-start(f32[512,8192]{1,0:T(8,128)S(1)} %get-tuple-element.228) | copy-start | bytes 50331652 | tf_op jit(solution)/shard_map/cond/branch_1_fun/while
  282.7 6.2 %copy-start = (f32[512,8192]{1,0:T(8,128)}, f32[512,8192]{1,0:T(8,128)S(1)}, u32[]{:S(2)}) copy-start(f32[512,8192]{1,0:T(8,128)S(1)} %get-tuple-element.228) | copy-start | bytes 50331652 | tf_op jit(solution)/shard_map/cond/branch_1_fun/while
  309.7 6.2 %copy-start = (f32[512,8192]{1,0:T(8,128)}, f32[512,8192]{1,0:T(8,128)S(1)}, u32[]{:S(2)}) copy-start(f32[512,8192]{1,0:T(8,128)S(1)} %get-tuple-element.228) | copy-start | bytes 50331652 | tf_op jit(solution)/shard_map/cond/branch_1_fun/while
  336.7 6.2 %copy-start = (f32[512,8192]{1,0:T(8,128)}, f32[512,8192]{1,0:T(8,128)S(1)}, u32[]{:S(2)}) copy-start(f32[512,8192]{1,0:T(8,128)S(1)} %get-tuple-element.228) | copy-start | bytes 50331652 | tf_op jit(solution)/shard_map/cond/branch_1_fun/while
Sparse Core Ops, SparseCore 0:
  30.3 37.7 all-gather.1
where the time goes:
time: 408 us; the launch traced here: 407 us
  matrix products  127 us (31%)
  other arithmetic  106 us (26%)
  local copies, waits for them, and re-layouts  62.7 us (15%)
  blocking collectives  50.7 us (12%)
  waiting for transfers between devices  24.6 us (6%)
  loops' own time  17.2 us (4%)
  between operations  14.8 us (4%)
    dot_general x8, matrix products, one_head(): jnp.dot(expo.astype(jnp.bfloat16), vh, preferred_element_type=jnp.float32)  72.5 us
    dot_general x8, matrix products, one_head(): scores = jnp.dot(qh, kh.T, preferred_element_type=jnp.float32) * scale  54.3 us
    unnamed x2, other arithmetic  51.8 us
    reduce_sum x8, other arithmetic, one_head(): summed = summed * factor + jnp.sum(expo, axis=1)  49.4 us
    all_to_all x1, blocking collectives, on_device(): lax.all_to_all(outputs, 'uly', split_axis=1, concat_axis=2, tiled=True)  31.7 us
    all_to_all x1, waiting for transfers between devices, on_device(): lax.all_to_all(queries, 'uly', split_axis=2, concat_axis=1, tiled=True)  24.5 us
    unnamed x13, local copies, waits for them, and re-layouts  20.5 us
    all_to_all x1, blocking collectives, side_by_side(): lax.all_to_all(both, axis, split_axis=split_dim, concat_axis=concat_dim,...  19.1 us
  transfers between devices with their start and end apart: 2, of which 1 were waited for; matrix products, arithmetic and copies ran while one was open for 18% of the time, Pallas kernels for 0%

commit v1 on v0

v1 whole, which is shorter than its diff:
```python
import jax
import jax.numpy as jnp
from jax import lax
from jax.experimental import pallas as pl
from jax.experimental.pallas import tpu as pltpu
from jax.sharding import Mesh, PartitionSpec as P

HEAD_WIDTH = 128
BLOCK = 128
CORES = 2
TILE = 512
LOG2E = 1.4426950408889634
SCALE = LOG2E * HEAD_WIDTH ** -0.5


def attention(where, docs, q, pieces):
    blocks, chunk, wide = q.shape
    heads = wide // HEAD_WIDTH
    rows = heads * chunk
    arrays = [p[0] for p in pieces]
    n = len(arrays)
    n_x = n // CORES
    block_tokens = n_x * chunk
    total = blocks * CORES * block_tokens
    n_docs = docs.shape[0]
    places = where

    def kernel(place, doc, q_ref, *refs):
        srcs, (o_ref, k_all, v_all, m_ref, l_ref, a_ref, sems) = refs[:n], refs[n:]
        step = pl.program_id(0)

        def copies():
            for i in range(n):
                at = place[2 + 2 * i]
                core = place[3 + 2 * i]
                for kind, dst in ((0, k_all), (1, v_all)):
                    yield pltpu.make_async_copy(
                        srcs[i].at[:, kind], dst.at[pl.ds(0, blocks), core, at], sems.at[kind, i]
                    )

        @pl.when(step == 0)
        def _():
            for c in copies():
                c.start()
            k_all[blocks, 0] = jnp.zeros((n_x, chunk, HEAD_WIDTH), jnp.bfloat16)
            v_all[blocks, 0] = jnp.zeros((n_x, chunk, HEAD_WIDTH), jnp.bfloat16)
            for c in copies():
                c.wait()

        first = (step * CORES + place[1]) * block_tokens + place[0] * chunk
        begin = jnp.int32(0)
        end = jnp.int32(0)
        for i in range(n_docs):
            end = end + doc[i] * BLOCK
            begin = jnp.where(end <= first, end, begin)
        span = first + chunk - begin
        tiles = (span + TILE - 1) // TILE

        m_ref[...] = jnp.full_like(m_ref, -1e30)
        l_ref[...] = jnp.zeros_like(l_ref)
        a_ref[...] = jnp.zeros_like(a_ref)
        qv = q_ref[0]
        qs = jnp.concatenate(
            [qv[:, h * HEAD_WIDTH : (h + 1) * HEAD_WIDTH] for h in range(heads)], axis=0
        )

        def tile(t, masked):
            at = begin // chunk + t * (TILE // chunk)
            kf = k_all.reshape((blocks + 1) * CORES * n_x, chunk, HEAD_WIDTH)
            vf = v_all.reshape((blocks + 1) * CORES * n_x, chunk, HEAD_WIDTH)
            kt = kf[pl.ds(at, TILE // chunk)].reshape(TILE, HEAD_WIDTH)
            vt = vf[pl.ds(at, TILE // chunk)].reshape(TILE, HEAD_WIDTH)
            s = lax.dot_general(qs, kt, (((1,), (1,)), ((), ())), preferred_element_type=jnp.float32)
            if masked:
                col = lax.broadcasted_iota(jnp.int32, (rows, TILE), 1) + (begin + t * TILE - first)
                row = lax.broadcasted_iota(jnp.int32, (rows, TILE), 0) & (chunk - 1)
                s = jnp.where(col <= row, s, -1e30)
            old = m_ref[...]
            new = jnp.maximum(old, jnp.max(s, axis=1, keepdims=True))
            alpha = jnp.exp2((old - new) * SCALE)
            p = [
                jnp.exp2((s[:, i : i + 128] - new) * SCALE) for i in range(0, TILE, 128)
            ]
            m_ref[...] = new
            l_ref[...] = l_ref[...] * alpha + sum(p[1:], p[0])
            pb = jnp.concatenate([x.astype(jnp.bfloat16) for x in p], axis=1)
            a_ref[...] = a_ref[...] * alpha + jnp.dot(pb, vt, preferred_element_type=jnp.float32)

        @pl.loop(0, tiles - 1)
        def _(t):
            tile(t, False)

        tile(tiles - 1, True)
        out = (a_ref[...] / jnp.sum(l_ref[...], axis=1, keepdims=True)).astype(jnp.bfloat16)
        for h in range(heads):
            o_ref[0, :, h * HEAD_WIDTH : (h + 1) * HEAD_WIDTH] = out[h * chunk : (h + 1) * chunk]

    smem = pl.BlockSpec(memory_space=pltpu.SMEM)
    hbm = pl.BlockSpec(memory_space=pltpu.HBM)
    row_spec = pl.BlockSpec((1, chunk, wide), lambda i: (i, 0, 0))
    return pl.pallas_call(
        kernel,
        grid=(blocks,),
        in_specs=[smem, smem, row_spec] + [hbm] * n,
        out_specs=row_spec,
        out_shape=jax.ShapeDtypeStruct(q.shape, jnp.bfloat16),
        scratch_shapes=[
            pltpu.VMEM((blocks + 1, CORES, n_x, chunk, HEAD_WIDTH), jnp.bfloat16),
            pltpu.VMEM((blocks + 1, CORES, n_x, chunk, HEAD_WIDTH), jnp.bfloat16),
            pltpu.VMEM((rows, HEAD_WIDTH), jnp.float32),
            pltpu.VMEM((rows, HEAD_WIDTH), jnp.float32),
            pltpu.VMEM((rows, HEAD_WIDTH), jnp.float32),
            pltpu.SemaphoreType.DMA((2, n)),
        ],
        compiler_params=pltpu.CompilerParams(dimension_semantics=("arbitrary",)),
    )(places, docs, q, *arrays)


def solution(mesh):
    parts, n_x, blk = mesh.devices.shape
    n_y = blk // CORES
    fine = Mesh(mesh.devices.reshape(parts, n_x, n_y, CORES), ("parts", "uly", "y", "core"))
    swap = [(2 * x + c, 2 * x + 1 - c) for x in range(n_x) for c in range(CORES)]
    ring = [
        (2 * x + c, 2 * ((x + 1 - 2 * c) % n_x) + c) for x in range(n_x) for c in range(CORES)
    ]

    def on_device(queries, keys, values, doc_blocks):
        x = lax.axis_index("uly")
        core = lax.axis_index("core")
        chunk = queries.shape[1]

        def by_head(a, wide):
            return jnp.transpose(a[0].reshape(chunk, n_y, wide), (1, 0, 2))

        kv = jnp.stack([by_head(keys, HEAD_WIDTH), by_head(values, HEAD_WIDTH)], axis=1)
        mine = lax.all_to_all(kv, "y", 0, 0, tiled=True)
        q = lax.all_to_all(by_head(queries, queries.shape[2] // n_y), "y", 0, 0, tiled=True)

        def step(a):
            return lax.ppermute(a, ("uly", "core"), ring)

        def other_core(a):
            return lax.ppermute(a, ("uly", "core"), swap)

        way = 1 - 2 * core
        other = other_core(mine)
        pieces = [(mine, x, core), (other, x, 1 - core)]
        m, o = mine, other
        for k in range(1, n_x // 2 + 1):
            here = (x - way * k) % n_x
            there = (x + way * k) % n_x
            m = step(m)
            pieces += [(m, here, core), (other_core(m), there, 1 - core)]
            if k < n_x // 2:
                o = step(o)
                pieces += [(o, here, 1 - core), (other_core(o), there, core)]
        where = jnp.stack([x, core] + [i for p in pieces for i in p[1:]]).astype(jnp.int32)
        heads = attention(where, doc_blocks, q, pieces)
        back = lax.all_to_all(heads, "y", 0, 0, tiled=True)
        return jnp.transpose(back, (1, 0, 2)).reshape(1, chunk, queries.shape[2])

    return jax.shard_map(
        on_device,
        mesh=fine,
        in_specs=(
            P(("parts", "y", "core"), "uly", None),
            P(("parts", "y", "core"), "uly", None),
            P(("parts", "y", "core"), "uly", None),
            P("parts"),
        ),
        out_specs=P(("parts", "y", "core"), "uly", None),
        check_vma=False,
    )
```

time: 408 us -> 133 us (0.33)
  the two profiles are of different devices: /device:TPU:720 before, /device:TPU:513 now
where the time goes in v1:
time: 133 us
  starting transfers between devices  51.1 us (38%)
  blocking collectives  34.3 us (26%)
  Pallas kernels  22.1 us (17%)
  waiting for transfers between devices  16.7 us (13%)
  local copies, waits for them, and re-layouts  7.74 us (6%)
    all_to_all x1, blocking collectives, on_device(): back = lax.all_to_all(heads, 'y', 0, 0, tiled=True)  34.3 us
    ppermute x8, starting transfers between devices, other_core(): return lax.ppermute(a, ('uly', 'core'), swap)  24.2 us
    pallas_call x1, Pallas kernels, attention(): pl.pallas_call(kernel, grid=(blocks,), in_specs=[smem, smem, row_spec] +...  22.1 us
    all_to_all x1, starting transfers between devices, on_device(): mine = lax.all_to_all(kv, 'y', 0, 0, tiled=True)  13.7 us
    ppermute x7, starting transfers between devices, step(): return lax.ppermute(a, ('uly', 'core'), ring)  9.49 us
    ppermute x7, waiting for transfers between devices, step(): return lax.ppermute(a, ('uly', 'core'), ring)  7.55 us
    all_to_all x1, waiting for transfers between devices, on_device(): mine = lax.all_to_all(kv, 'y', 0, 0, tiled=True)  7.17 us
    all_to_all x1, starting transfers between devices, on_device(): lax.all_to_all(by_head(queries, queries.shape[2] // n_y), 'y', 0, 0, tile...  3.76 us
  transfers between devices with their start and end apart: 17, of which 6 were waited for; matrix products, arithmetic and copies ran while one was open for 2% of the time, Pallas kernels for 0%

profile of v1, /device:TPU:513, one launch (start us, length us, event | category | flops | bytes accessed | tf_op | source)
XLA Modules:
  0.0 132.8 jit_solution(10814241955662563124)
XLA Ops:
  0.0 1.0 copy.11
  1.0 0.9 copy.10
  2.0 0.7 pad_maximum_fusion
  2.7 13.7 %all-to-all-start.1 = ((bf16[8,2,64,128]{3,2,1,0:T(8,128)(2,1)}), bf16[8,2,64,128]{3,2,1,0:T(8,128)(2,1)S(1)}, u32[]{:S(2)}, u32[]{:S(2)}) async-start(bf16[8,2,64,128]{3,2,1,0:T(8,128)(2,1)} %pad_maximum_fusion), calls=%async_computation.1 | async-start | bytes 524288 | tf_op jit(solution)/shard_map/all_to_all | solution.py:137
  16.4 0.0 copy-done.1
  16.4 0.6 copy.9
  17.0 1.5 %copy.15 = bf16[64,8,1024]{2,0,1:T(8,128)(2,1)} copy(bf16[64,8,1024]{2,1,0:T(8,128)(2,1)S(1)} %bitcast.33) | data formatting | bytes 2097152 | tf_op jit(solution)/shard_map/reshape;squeeze | solution.py:134
  18.6 7.2 %all-to-all-done.1.refs_0_ = bf16[8,2,64,128]{3,2,1,0:T(8,128)(2,1)S(1)} async-done(((bf16[8,2,64,128]{3,2,1,0:T(8,128)(2,1)}), bf16[8,2,64,128]{3,2,1,0:T(8,128)(2,1)S(1)}, u32[]{:S(2)}, u32[]{:S(2)}) %all-to-all-start.1) | async-done | bytes 262176 | tf_op jit(solution)/shard_map/all_to_all | solution.py:137
  25.8 3.8 %all-to-all-start = ((bf16[8,64,1024]{2,1,0:T(8,128)(2,1)}), bf16[8,64,1024]{2,1,0:T(8,128)(2,1)S(1)}, u32[]{:S(2)}, u32[]{:S(2)}) async-start(bf16[8,64,1024]{2,1,0:T(8,128)(2,1)} %bitcast.31), calls=%async_computation | async-start | bytes 2097152 | tf_op jit(solution)/shard_map/all_to_all | solution.py:138
  29.5 11.8 %collective-permute-start = (bf16[8,2,64,128]{3,2,1,0:T(8,128)(2,1)S(1)}, bf16[8,2,64,128]{3,2,1,0:T(8,128)(2,1)S(1)}, u32[]{:S(2)}, u32[]{:S(2)}) collective-permute-start(bf16[8,2,64,128]{3,2,1,0:T(8,128)(2,1)S(1)} %all-to-all-done.1.refs_0_), channel_id=1, source_target_pairs={{0,1},{1,0},{16,17},{17,16},{32,33},{33,32},{48,49},{49,48},{64,65... | collective-permute-start | bytes 786440 | tf_op jit(solution)/shard_map/ppermute | solution.py:144
  41.4 0.0 collective-permute-start.1
  41.4 1.2 collective-permute-done.refs_1_
  42.5 0.0 collective-permute-start.3
  42.5 4.4 %collective-permute-done.1.refs_2_ = bf16[8,2,64,128]{3,2,1,0:T(8,128)(2,1)S(1)} collective-permute-done((bf16[8,2,64,128]{3,2,1,0:T(8,128)(2,1)S(1)}, bf16[8,2,64,128]{3,2,1,0:T(8,128)(2,1)S(1)}, u32[]{:S(2)}, u32[]{:S(2)}) %collective-permute-start.1) | collective-permute-done | bytes 262176 | tf_op jit(solution)/shard_map/ppermute | solution.py:141
  46.9 1.2 collective-permute-start.5
  48.1 1.6 %collective-permute-done.3.refs_4_ = bf16[8,2,64,128]{3,2,1,0:T(8,128)(2,1)S(1)} collective-permute-done((bf16[8,2,64,128]{3,2,1,0:T(8,128)(2,1)S(1)}, bf16[8,2,64,128]{3,2,1,0:T(8,128)(2,1)S(1)}, u32[]{:S(2)}, u32[]{:S(2)}) %collective-permute-start.3) | collective-permute-done | bytes 262176 | tf_op jit(solution)/shard_map/ppermute | solution.py:141
  49.7 1.2 collective-permute-start.7
  50.9 1.6 %collective-permute-done.5.refs_6_ = bf16[8,2,64,128]{3,2,1,0:T(8,128)(2,1)S(1)} collective-permute-done((bf16[8,2,64,128]{3,2,1,0:T(8,128)(2,1)S(1)}, bf16[8,2,64,128]{3,2,1,0:T(8,128)(2,1)S(1)}, u32[]{:S(2)}, u32[]{:S(2)}) %collective-permute-start.5) | collective-permute-done | bytes 262176 | tf_op jit(solution)/shard_map/ppermute | solution.py:141
  52.5 2.3 %collective-permute-start.9 = (bf16[8,2,64,128]{3,2,1,0:T(8,128)(2,1)S(1)}, bf16[8,2,64,128]{3,2,1,0:T(8,128)(2,1)S(1)}, u32[]{:S(2)}, u32[]{:S(2)}) collective-permute-start(bf16[8,2,64,128]{3,2,1,0:T(8,128)(2,1)S(1)} %collective-permute-done.5.refs_6_), channel_id=1, source_target_pairs={{0,16},{1,113},{16,32},{17,1},{32,48},{33,17},{48,64},{49,33},{64,... | collective-permute-start | bytes 786440 | tf_op jit(solution)/shard_map/ppermute | solution.py:141
  54.8 1.9 %collective-permute-start.2 = (bf16[8,2,64,128]{3,2,1,0:T(8,128)(2,1)S(1)}, bf16[8,2,64,128]{3,2,1,0:T(8,128)(2,1)S(1)}, u32[]{:S(2)}, u32[]{:S(2)}) collective-permute-start(bf16[8,2,64,128]{3,2,1,0:T(8,128)(2,1)S(1)} %collective-permute-done.1.refs_2_), channel_id=1, source_target_pairs={{0,1},{1,0},{16,17},{17,16},{32,33},{33,32},{48,49},{49,48},{64,65... | collective-permute-start | bytes 786440 | tf_op jit(solution)/shard_map/ppermute | solution.py:144
  56.7 0.1 collective-permute-start.4
  56.8 0.0 collective-permute-done.7.refs_8_
  56.8 2.9 %collective-permute-start.11 = (bf16[8,2,64,128]{3,2,1,0:T(8,128)(2,1)S(1)}, bf16[8,2,64,128]{3,2,1,0:T(8,128)(2,1)S(1)}, u32[]{:S(2)}, u32[]{:S(2)}) collective-permute-start(bf16[8,2,64,128]{3,2,1,0:T(8,128)(2,1)S(1)} %collective-permute-done.7.refs_8_), channel_id=1, source_target_pairs={{0,16},{1,113},{16,32},{17,1},{32,48},{33,17},{48,64},{49,33},{64,... | collective-permute-start | bytes 786440 | tf_op jit(solution)/shard_map/ppermute | solution.py:141
  59.8 0.0 collective-permute-done.9.refs_10_
  59.8 1.8 %collective-permute-start.13 = (bf16[8,2,64,128]{3,2,1,0:T(8,128)(2,1)S(1)}, bf16[8,2,64,128]{3,2,1,0:T(8,128)(2,1)}, u32[]{:S(2)}, u32[]{:S(2)}) collective-permute-start(bf16[8,2,64,128]{3,2,1,0:T(8,128)(2,1)S(1)} %collective-permute-done.9.refs_10_), channel_id=1, source_target_pairs={{0,16},{1,113},{16,32},{17,1},{32,48},{33,17},{48,64},{49,33},{64,... | collective-permute-start | bytes 786440 | tf_op jit(solution)/shard_map/ppermute | solution.py:141
  61.6 2.7 %collective-permute-start.6 = (bf16[8,2,64,128]{3,2,1,0:T(8,128)(2,1)S(1)}, bf16[8,2,64,128]{3,2,1,0:T(8,128)(2,1)}, u32[]{:S(2)}, u32[]{:S(2)}) collective-permute-start(bf16[8,2,64,128]{3,2,1,0:T(8,128)(2,1)S(1)} %collective-permute-done.5.refs_6_), channel_id=1, source_target_pairs={{0,1},{1,0},{16,17},{17,16},{32,33},{33,32},{48,49},{49,48},{64,65... | collective-permute-start | bytes 786440 | tf_op jit(solution)/shard_map/ppermute | solution.py:144
  64.3 0.0 collective-permute-done.2.refs_3_
  64.3 0.1 collective-permute-start.8
  64.4 0.0 collective-permute-done.4.refs_5_
  64.4 0.4 collective-permute-start.10
  64.8 0.0 collective-permute-done.11.refs_12_
  64.8 2.3 %collective-permute-start.12 = (bf16[8,2,64,128]{3,2,1,0:T(8,128)(2,1)S(1)}, bf16[8,2,64,128]{3,2,1,0:T(8,128)(2,1)}, u32[]{:S(2)}, u32[]{:S(2)}) collective-permute-start(bf16[8,2,64,128]{3,2,1,0:T(8,128)(2,1)S(1)} %collective-permute-done.11.refs_12_), channel_id=1, source_target_pairs={{0,1},{1,0},{16,17},{17,16},{32,33},{33,32},{48,49},{49,48},{64,65... | collective-permute-start | bytes 786440 | tf_op jit(solution)/shard_map/ppermute | solution.py:144
  67.1 0.0 collective-permute-done.13.refs_14_
  67.1 4.9 %collective-permute-start.14 = (bf16[8,2,64,128]{3,2,1,0:T(8,128)(2,1)}, bf16[8,2,64,128]{3,2,1,0:T(8,128)(2,1)}, u32[]{:S(2)}, u32[]{:S(2)}) collective-permute-start(bf16[8,2,64,128]{3,2,1,0:T(8,128)(2,1)} %collective-permute-done.13.refs_14_), channel_id=1, source_target_pairs={{0,1},{1,0},{16,17},{17,16},{32,33},{33,32},{48,49},{49,48},{64,65... | collective-permute-start | bytes 786440 | tf_op jit(solution)/shard_map/ppermute | solution.py:144
  72.0 0.7 stack.79.place
  72.7 0.0 collective-permute-done.6.refs_7_
  72.7 0.0 collective-permute-done.8.refs_9_
  72.7 0.0 collective-permute-done.10.refs_11_
  72.7 0.0 collective-permute-done.12.refs_13_
  72.7 0.8 collective-permute-done.14.refs_15_
  73.5 0.0 all-to-all-done.q_ref
  73.5 0.0 copy-done.5
  73.5 0.0 copy-start
  73.6 1.0 copy-done
  74.5 22.1 %shard_map.46 = bf16[8,64,1024]{2,1,0:T(8,128)(2,1)} custom-call(s32[34]{0:T(128)} %stack.79.place, s32[16]{0:T(128)} %doc.1, bf16[8,64,1024]{2,1,0:T(8,128)(2,1)} %copy-done, bf16[8,2,64,128]{3,2,1,0:T(8,128)(2,1)} %copy-done.2, bf16[8,2,64,128]{3,2,1,0:T(8,128)(2,1)} %copy-done.3, bf16[8,2,64,128]{3,2,1,0:T(8,128)(2,1)} %copy-done.4, ...), custom_call_target="tpu_custom_call" | custom-call | tf_op jit(solution)/shard_map/pallas_call | solution.py:101
  96.6 34.3 %all_to_all.15 = bf16[8,64,1024]{2,1,0:T(8,128)(2,1)S(1)} all-to-all(bf16[8,64,1024]{2,1,0:T(8,128)(2,1)} %shard_map.46), channel_id=1, replica_groups=mesh['parts'=2,'uly'=8,'y'=8,'core'=2] {'y'}, dimensions={0} | all-to-all | bytes 2097152 | tf_op jit(solution)/shard_map/all_to_all | solution.py:160
  131.0 0.6 copy.8
  131.5 1.3 reshape.3
  (21 shorter events, 0.1 us)
Async XLA Ops:
  0.0 16.4 %copy-start.1 = (bf16[1,64,8192]{2,1,0:T(8,128)(2,1)S(1)}, bf16[1,64,8192]{2,1,0:T(8,128)(2,1)}, u32[]{:S(2)}) copy-start(bf16[1,64,8192]{2,1,0:T(8,128)(2,1)} %param.4) | copy-start | bytes 3145732
  2.7 23.0 %all-to-all-start.1 = ((bf16[8,2,64,128]{3,2,1,0:T(8,128)(2,1)}), bf16[8,2,64,128]{3,2,1,0:T(8,128)(2,1)S(1)}, u32[]{:S(2)}, u32[]{:S(2)}) async-start(bf16[8,2,64,128]{3,2,1,0:T(8,128)(2,1)} %pad_maximum_fusion), calls=%async_computation.1 | async-start | bytes 524288 | tf_op jit(solution)/shard_map/all_to_all | solution.py:137
  25.8 15.6 %copy-start.2 = (bf16[8,2,64,128]{3,2,1,0:T(8,128)(2,1)}, bf16[8,2,64,128]{3,2,1,0:T(8,128)(2,1)S(1)}, u32[]{:S(2)}) copy-start(bf16[8,2,64,128]{3,2,1,0:T(8,128)(2,1)S(1)} %all-to-all-done.1.refs_0_) | copy-start | bytes 786436
  25.8 47.7 %all-to-all-start = ((bf16[8,64,1024]{2,1,0:T(8,128)(2,1)}), bf16[8,64,1024]{2,1,0:T(8,128)(2,1)S(1)}, u32[]{:S(2)}, u32[]{:S(2)}) async-start(bf16[8,64,1024]{2,1,0:T(8,128)(2,1)} %bitcast.31), calls=%async_computation | async-start | bytes 2097152 | tf_op jit(solution)/shard_map/all_to_all | solution.py:138
  29.5 13.0 %collective-permute-start = (bf16[8,2,64,128]{3,2,1,0:T(8,128)(2,1)S(1)}, bf16[8,2,64,128]{3,2,1,0:T(8,128)(2,1)S(1)}, u32[]{:S(2)}, u32[]{:S(2)}) collective-permute-start(bf16[8,2,64,128]{3,2,1,0:T(8,128)(2,1)S(1)} %all-to-all-done.1.refs_0_), channel_id=1, source_target_pairs={{0,1},{1,0},{16,17},{17,16},{32,33},{33,32},{48,49},{49,48},{64,65... | collective-permute-start | bytes 786440 | tf_op jit(solution)/shard_map/ppermute | solution.py:144
  41.4 5.5 %collective-permute-start.1 = (bf16[8,2,64,128]{3,2,1,0:T(8,128)(2,1)S(1)}, bf16[8,2,64,128]{3,2,1,0:T(8,128)(2,1)S(1)}, u32[]{:S(2)}, u32[]{:S(2)}) collective-permute-start(bf16[8,2,64,128]{3,2,1,0:T(8,128)(2,1)S(1)} %all-to-all-done.1.refs_0_), channel_id=1, source_target_pairs={{0,16},{1,113},{16,32},{17,1},{32,48},{33,17},{48,64},{49,33},{64,... | collective-permute-start | bytes 786440 | tf_op jit(solution)/shard_map/ppermute | solution.py:141
  42.5 30.9 %copy-start.3 = (bf16[8,2,64,128]{3,2,1,0:T(8,128)(2,1)}, bf16[8,2,64,128]{3,2,1,0:T(8,128)(2,1)S(1)}, u32[]{:S(2)}) copy-start(bf16[8,2,64,128]{3,2,1,0:T(8,128)(2,1)S(1)} %collective-permute-done.refs_1_) | copy-start | bytes 786436
  42.5 7.2 %collective-permute-start.3 = (bf16[8,2,64,128]{3,2,1,0:T(8,128)(2,1)S(1)}, bf16[8,2,64,128]{3,2,1,0:T(8,128)(2,1)S(1)}, u32[]{:S(2)}, u32[]{:S(2)}) collective-permute-start(bf16[8,2,64,128]{3,2,1,0:T(8,128)(2,1)S(1)} %collective-permute-done.refs_1_), channel_id=1, source_target_pairs={{0,16},{1,113},{16,32},{17,1},{32,48},{33,17},{48,64},{49,33},{64,... | collective-permute-start | bytes 786440 | tf_op jit(solution)/shard_map/ppermute | solution.py:141
  46.9 26.6 %copy-start.4 = (bf16[8,2,64,128]{3,2,1,0:T(8,128)(2,1)}, bf16[8,2,64,128]{3,2,1,0:T(8,128)(2,1)S(1)}, u32[]{:S(2)}) copy-start(bf16[8,2,64,128]{3,2,1,0:T(8,128)(2,1)S(1)} %collective-permute-done.1.refs_2_) | copy-start | bytes 786436
  46.9 5.6 %collective-permute-start.5 = (bf16[8,2,64,128]{3,2,1,0:T(8,128)(2,1)S(1)}, bf16[8,2,64,128]{3,2,1,0:T(8,128)(2,1)S(1)}, u32[]{:S(2)}, u32[]{:S(2)}) collective-permute-start(bf16[8,2,64,128]{3,2,1,0:T(8,128)(2,1)S(1)} %collective-permute-done.1.refs_2_), channel_id=1, source_target_pairs={{0,16},{1,113},{16,32},{17,1},{32,48},{33,17},{48,64},{49,33},{64,... | collective-permute-start | bytes 786440 | tf_op jit(solution)/shard_map/ppermute | solution.py:141
  49.7 23.8 %copy-start.5 = (bf16[8,2,64,128]{3,2,1,0:T(8,128)(2,1)}, bf16[8,2,64,128]{3,2,1,0:T(8,128)(2,1)S(1)}, u32[]{:S(2)}) copy-start(bf16[8,2,64,128]{3,2,1,0:T(8,128)(2,1)S(1)} %collective-permute-done.3.refs_4_) | copy-start | bytes 786436
  49.7 7.1 %collective-permute-start.7 = (bf16[8,2,64,128]{3,2,1,0:T(8,128)(2,1)S(1)}, bf16[8,2,64,128]{3,2,1,0:T(8,128)(2,1)S(1)}, u32[]{:S(2)}, u32[]{:S(2)}) collective-permute-start(bf16[8,2,64,128]{3,2,1,0:T(8,128)(2,1)S(1)} %collective-permute-done.3.refs_4_), channel_id=1, source_target_pairs={{0,16},{1,113},{16,32},{17,1},{32,48},{33,17},{48,64},{49,33},{64,... | collective-permute-start | bytes 786440 | tf_op jit(solution)/shard_map/ppermute | solution.py:141
  52.5 21.0 %copy-start.6 = (bf16[8,2,64,128]{3,2,1,0:T(8,128)(2,1)}, bf16[8,2,64,128]{3,2,1,0:T(8,128)(2,1)S(1)}, u32[]{:S(2)}) copy-start(bf16[8,2,64,128]{3,2,1,0:T(8,128)(2,1)S(1)} %collective-permute-done.5.refs_6_) | copy-start | bytes 786436
  52.5 7.3 %collective-permute-start.9 = (bf16[8,2,64,128]{3,2,1,0:T(8,128)(2,1)S(1)}, bf16[8,2,64,128]{3,2,1,0:T(8,128)(2,1)S(1)}, u32[]{:S(2)}, u32[]{:S(2)}) collective-permute-start(bf16[8,2,64,128]{3,2,1,0:T(8,128)(2,1)S(1)} %collective-permute-done.5.refs_6_), channel_id=1, source_target_pairs={{0,16},{1,113},{16,32},{17,1},{32,48},{33,17},{48,64},{49,33},{64,... | collective-permute-start | bytes 786440 | tf_op jit(solution)/shard_map/ppermute | solution.py:141
  54.8 9.4 %collective-permute-start.2 = (bf16[8,2,64,128]{3,2,1,0:T(8,128)(2,1)S(1)}, bf16[8,2,64,128]{3,2,1,0:T(8,128)(2,1)S(1)}, u32[]{:S(2)}, u32[]{:S(2)}) collective-permute-start(bf16[8,2,64,128]{3,2,1,0:T(8,128)(2,1)S(1)} %collective-permute-done.1.refs_2_), channel_id=1, source_target_pairs={{0,1},{1,0},{16,17},{17,16},{32,33},{33,32},{48,49},{49,48},{64,65... | collective-permute-start | bytes 786440 | tf_op jit(solution)/shard_map/ppermute | solution.py:144
  56.7 7.7 %collective-permute-start.4 = (bf16[8,2,64,128]{3,2,1,0:T(8,128)(2,1)S(1)}, bf16[8,2,64,128]{3,2,1,0:T(8,128)(2,1)S(1)}, u32[]{:S(2)}, u32[]{:S(2)}) collective-permute-start(bf16[8,2,64,128]{3,2,1,0:T(8,128)(2,1)S(1)} %collective-permute-done.3.refs_4_), channel_id=1, source_target_pairs={{0,1},{1,0},{16,17},{17,16},{32,33},{33,32},{48,49},{49,48},{64,65... | collective-permute-start | bytes 786440 | tf_op jit(solution)/shard_map/ppermute | solution.py:144
  56.8 16.7 %copy-start.7 = (bf16[8,2,64,128]{3,2,1,0:T(8,128)(2,1)}, bf16[8,2,64,128]{3,2,1,0:T(8,128)(2,1)S(1)}, u32[]{:S(2)}) copy-start(bf16[8,2,64,128]{3,2,1,0:T(8,128)(2,1)S(1)} %collective-permute-done.7.refs_8_) | copy-start | bytes 786436
  56.8 8.0 %collective-permute-start.11 = (bf16[8,2,64,128]{3,2,1,0:T(8,128)(2,1)S(1)}, bf16[8,2,64,128]{3,2,1,0:T(8,128)(2,1)S(1)}, u32[]{:S(2)}, u32[]{:S(2)}) collective-permute-start(bf16[8,2,64,128]{3,2,1,0:T(8,128)(2,1)S(1)} %collective-permute-done.7.refs_8_), channel_id=1, source_target_pairs={{0,16},{1,113},{16,32},{17,1},{32,48},{33,17},{48,64},{49,33},{64,... | collective-permute-start | bytes 786440 | tf_op jit(solution)/shard_map/ppermute | solution.py:141
  59.8 13.7 %copy-start.8 = (bf16[8,2,64,128]{3,2,1,0:T(8,128)(2,1)}, bf16[8,2,64,128]{3,2,1,0:T(8,128)(2,1)S(1)}, u32[]{:S(2)}) copy-start(bf16[8,2,64,128]{3,2,1,0:T(8,128)(2,1)S(1)} %collective-permute-done.9.refs_10_) | copy-start | bytes 786436
  59.8 7.3 %collective-permute-start.13 = (bf16[8,2,64,128]{3,2,1,0:T(8,128)(2,1)S(1)}, bf16[8,2,64,128]{3,2,1,0:T(8,128)(2,1)}, u32[]{:S(2)}, u32[]{:S(2)}) collective-permute-start(bf16[8,2,64,128]{3,2,1,0:T(8,128)(2,1)S(1)} %collective-permute-done.9.refs_10_), channel_id=1, source_target_pairs={{0,16},{1,113},{16,32},{17,1},{32,48},{33,17},{48,64},{49,33},{64,... | collective-permute-start | bytes 786440 | tf_op jit(solution)/shard_map/ppermute | solution.py:141
  61.6 11.1 %collective-permute-start.6 = (bf16[8,2,64,128]{3,2,1,0:T(8,128)(2,1)S(1)}, bf16[8,2,64,128]{3,2,1,0:T(8,128)(2,1)}, u32[]{:S(2)}, u32[]{:S(2)}) collective-permute-start(bf16[8,2,64,128]{3,2,1,0:T(8,128)(2,1)S(1)} %collective-permute-done.5.refs_6_), channel_id=1, source_target_pairs={{0,1},{1,0},{16,17},{17,16},{32,33},{33,32},{48,49},{49,48},{64,65... | collective-permute-start | bytes 786440 | tf_op jit(solution)/shard_map/ppermute | solution.py:144
  64.3 9.2 %copy-start.9 = (bf16[8,2,64,128]{3,2,1,0:T(8,128)(2,1)}, bf16[8,2,64,128]{3,2,1,0:T(8,128)(2,1)S(1)}, u32[]{:S(2)}) copy-start(bf16[8,2,64,128]{3,2,1,0:T(8,128)(2,1)S(1)} %collective-permute-done.2.refs_3_) | copy-start | bytes 786436
  64.3 8.4 %collective-permute-start.8 = (bf16[8,2,64,128]{3,2,1,0:T(8,128)(2,1)S(1)}, bf16[8,2,64,128]{3,2,1,0:T(8,128)(2,1)}, u32[]{:S(2)}, u32[]{:S(2)}) collective-permute-start(bf16[8,2,64,128]{3,2,1,0:T(8,128)(2,1)S(1)} %collective-permute-done.7.refs_8_), channel_id=1, source_target_pairs={{0,1},{1,0},{16,17},{17,16},{32,33},{33,32},{48,49},{49,48},{64,65... | collective-permute-start | bytes 786440 | tf_op jit(solution)/shard_map/ppermute | solution.py:144
  64.4 9.1 %copy-start.10 = (bf16[8,2,64,128]{3,2,1,0:T(8,128)(2,1)}, bf16[8,2,64,128]{3,2,1,0:T(8,128)(2,1)S(1)}, u32[]{:S(2)}) copy-start(bf16[8,2,64,128]{3,2,1,0:T(8,128)(2,1)S(1)} %collective-permute-done.4.refs_5_) | copy-start | bytes 786436
  64.4 8.3 %collective-permute-start.10 = (bf16[8,2,64,128]{3,2,1,0:T(8,128)(2,1)S(1)}, bf16[8,2,64,128]{3,2,1,0:T(8,128)(2,1)}, u32[]{:S(2)}, u32[]{:S(2)}) collective-permute-start(bf16[8,2,64,128]{3,2,1,0:T(8,128)(2,1)S(1)} %collective-permute-done.9.refs_10_), channel_id=1, source_target_pairs={{0,1},{1,0},{16,17},{17,16},{32,33},{33,32},{48,49},{49,48},{64,65... | collective-permute-start | bytes 786440 | tf_op jit(solution)/shard_map/ppermute | solution.py:144
  64.8 8.7 %copy-start.11 = (bf16[8,2,64,128]{3,2,1,0:T(8,128)(2,1)}, bf16[8,2,64,128]{3,2,1,0:T(8,128)(2,1)S(1)}, u32[]{:S(2)}) copy-start(bf16[8,2,64,128]{3,2,1,0:T(8,128)(2,1)S(1)} %collective-permute-done.11.refs_12_) | copy-start | bytes 786436
  64.8 7.9 %collective-permute-start.12 = (bf16[8,2,64,128]{3,2,1,0:T(8,128)(2,1)S(1)}, bf16[8,2,64,128]{3,2,1,0:T(8,128)(2,1)}, u32[]{:S(2)}, u32[]{:S(2)}) collective-permute-start(bf16[8,2,64,128]{3,2,1,0:T(8,128)(2,1)S(1)} %collective-permute-done.11.refs_12_), channel_id=1, source_target_pairs={{0,1},{1,0},{16,17},{17,16},{32,33},{33,32},{48,49},{49,48},{64,65... | collective-permute-start | bytes 786440 | tf_op jit(solution)/shard_map/ppermute | solution.py:144
  67.1 6.4 %collective-permute-start.14 = (bf16[8,2,64,128]{3,2,1,0:T(8,128)(2,1)}, bf16[8,2,64,128]{3,2,1,0:T(8,128)(2,1)}, u32[]{:S(2)}, u32[]{:S(2)}) collective-permute-start(bf16[8,2,64,128]{3,2,1,0:T(8,128)(2,1)} %collective-permute-done.13.refs_14_), channel_id=1, source_target_pairs={{0,1},{1,0},{16,17},{17,16},{32,33},{33,32},{48,49},{49,48},{64,65... | collective-permute-start | bytes 786440 | tf_op jit(solution)/shard_map/ppermute | solution.py:144
  73.5 1.0 copy-start

commit v2 on v1

v2 whole, which is shorter than its diff:
```python
import jax
import jax.numpy as jnp
from jax import lax
from jax.experimental import pallas as pl
from jax.experimental.pallas import tpu as pltpu
from jax.sharding import Mesh, PartitionSpec as P


HEAD_WIDTH = 128
BLOCK = 128
CORES = 2
TILE = 1024
SPLIT = 2
LATE = 0
VMEM_LIMIT = 32 << 20
LOG2E = 1.4426950408889634
SCALE = LOG2E * HEAD_WIDTH ** -0.5


def in_vmem(a):
    return pltpu.with_memory_space_constraint(a, pltpu.VMEM)


def in_hbm(a):
    return pltpu.with_memory_space_constraint(a, pltpu.HBM)


def attention(docs, q, pieces):
    blocks, chunk, wide = q.shape
    heads = wide // HEAD_WIDTH
    rows = heads * chunk
    arrays = [p[0] for p in pieces]
    n = len(arrays)
    n_x = n // CORES
    block_tokens = n_x * chunk
    total = blocks * CORES * block_tokens
    n_docs = docs.shape[0]
    part = rows // SPLIT

    def kernel(doc, q_ref, *refs):
        srcs, (o_ref, k_all, v_all, q_s, m_ref, a_ref, sems) = refs[:n], refs[n:]
        x = lax.axis_index("uly")
        core = lax.axis_index("core")
        way = 1 - 2 * core
        k_pieces = k_all.reshape(blocks + TILE // (CORES * block_tokens), CORES, n_x, chunk, HEAD_WIDTH)
        v_pieces = v_all.reshape(blocks + TILE // (CORES * block_tokens), CORES, n_x, chunk, HEAD_WIDTH)
        copies = []
        for i in range(n):
            at = (x - way * pieces[i][1]) % n_x
            of = core + pieces[i][2] * way
            for kind, dst in ((0, k_pieces), (1, v_pieces)):
                if i < n - LATE:
                    copies.append(
                        pltpu.make_async_copy(
                            srcs[i].at[:, kind], dst.at[pl.ds(0, blocks), of, at], sems.at[kind, i]
                        )
                    )
                    copies[-1].start()
                else:
                    for b in range(blocks):
                        dst[b, of, at] = srcs[i][b, kind]
        k_all[total:] = jnp.zeros((TILE, HEAD_WIDTH), jnp.bfloat16)
        v_all[total:] = jnp.zeros((TILE, HEAD_WIDTH), jnp.bfloat16)
        ones = jnp.ones((TILE, HEAD_WIDTH), jnp.bfloat16)
        for c in copies:
            c.wait()

        @pl.loop(0, blocks)
        def _(step):
            first = (step * CORES + core) * block_tokens + x * chunk
            begin = jnp.int32(0)
            end = jnp.int32(0)
            for i in range(n_docs):
                end = end + doc[i] * BLOCK
                begin = jnp.where(end <= first, end, begin)
            tiles = (first + chunk - begin + TILE - 1) // TILE
            for h in range(heads):
                q_s[h * chunk : (h + 1) * chunk] = q_ref[step, :, h * HEAD_WIDTH : (h + 1) * HEAD_WIDTH]
            m_ref[...] = jnp.full_like(m_ref, -1e30)
            a_ref[...] = jnp.zeros_like(a_ref)

            def tile(t, masked):
                at = pl.multiple_of(begin + t * TILE, BLOCK)
                kt = k_all[pl.ds(at, TILE)]
                vt = jnp.concatenate([v_all[pl.ds(at, TILE)], ones], axis=1)
                for g in range(SPLIT):
                    some = slice(g * part, (g + 1) * part)
                    s = lax.dot_general(
                        q_s[some], kt, (((1,), (1,)), ((), ())), preferred_element_type=jnp.float32
                    )
                    if masked:
                        col = lax.broadcasted_iota(jnp.int32, (part, TILE), 1) + (at - first)
                        row = lax.broadcasted_iota(jnp.int32, (part, TILE), 0) & (chunk - 1)
                        s = jnp.where(col <= row, s, -1e30)
                    old = m_ref[some]
                    new = jnp.maximum(old, jnp.max(s, axis=1, keepdims=True))
                    alpha = jnp.exp2((old - new) * SCALE)
                    m_ref[some] = new
                    p = jnp.concatenate(
                        [
                            jnp.exp2((s[:, i : i + 128] - new) * SCALE).astype(jnp.bfloat16)
                            for i in range(0, TILE, 128)
                        ],
                        axis=1,
                    )
                    d = jnp.dot(p, vt, preferred_element_type=jnp.float32)
                    for c in range(0, 2 * HEAD_WIDTH, HEAD_WIDTH):
                        here = slice(c, c + HEAD_WIDTH)
                        a_ref[some, here] = a_ref[some, here] * alpha + d[:, here]

            @pl.loop(0, tiles - 1)
            def _(t):
                tile(t, False)

            tile(tiles - 1, True)
            for h in range(heads):
                of = slice(h * chunk, (h + 1) * chunk)
                o_ref[step, :, h * HEAD_WIDTH : (h + 1) * HEAD_WIDTH] = (
                    a_ref[of, :HEAD_WIDTH] / a_ref[of, HEAD_WIDTH:]
                ).astype(jnp.bfloat16)

    smem = pl.BlockSpec(memory_space=pltpu.SMEM)
    hbm = pl.BlockSpec(memory_space=pltpu.HBM)
    vmem = pl.BlockSpec(memory_space=pltpu.VMEM)
    return pl.pallas_call(
        kernel,
        in_specs=[smem, vmem] + [hbm] * (n - LATE) + [vmem] * LATE,
        out_specs=vmem,
        out_shape=pltpu.VMEM(q.shape, jnp.bfloat16),
        scratch_shapes=[
            pltpu.VMEM((total + TILE, HEAD_WIDTH), jnp.bfloat16),
            pltpu.VMEM((total + TILE, HEAD_WIDTH), jnp.bfloat16),
            pltpu.VMEM((rows, HEAD_WIDTH), jnp.bfloat16),
            pltpu.VMEM((rows, HEAD_WIDTH), jnp.float32),
            pltpu.VMEM((rows, 2 * HEAD_WIDTH), jnp.float32),
            pltpu.SemaphoreType.DMA((2, n)),
        ],
        compiler_params=pltpu.CompilerParams(vmem_limit_bytes=VMEM_LIMIT),
    )(docs, in_vmem(q), *[in_hbm(a) for a in arrays[: n - LATE]], *[in_vmem(a) for a in arrays[n - LATE :]])


def by_head(keys, values, heads):
    chunk = keys.shape[1]

    def kernel(k_ref, v_ref, o_ref):
        for h in range(heads):
            o_ref[h, 0] = k_ref[0, :, h * HEAD_WIDTH : (h + 1) * HEAD_WIDTH]
            o_ref[h, 1] = v_ref[0, :, h * HEAD_WIDTH : (h + 1) * HEAD_WIDTH]

    vmem = pl.BlockSpec(memory_space=pltpu.VMEM)
    return pl.pallas_call(
        kernel,
        in_specs=[vmem, vmem],
        out_specs=vmem,
        out_shape=pltpu.VMEM((heads, 2, chunk, HEAD_WIDTH), keys.dtype),
    )(keys, values)


def side_by_side(a):
    groups, chunk, wide = a.shape

    def kernel(a_ref, o_ref, sems):
        copies = [
            pltpu.make_async_copy(a_ref.at[g], o_ref.at[0, :, pl.ds(g * wide, wide)], sems.at[g])
            for g in range(groups)
        ]
        for c in copies:
            c.start()
        for c in copies:
            c.wait()

    return pl.pallas_call(
        kernel,
        in_specs=[pl.BlockSpec(memory_space=pltpu.VMEM)],
        out_specs=pl.BlockSpec(memory_space=pltpu.HBM),
        out_shape=jax.ShapeDtypeStruct((1, chunk, groups * wide), a.dtype),
        scratch_shapes=[pltpu.SemaphoreType.DMA((groups,))],
    )(in_vmem(a))


def solution(mesh):
    parts, n_x, blk = mesh.devices.shape
    n_y = blk // CORES
    fine = Mesh(mesh.devices.reshape(parts, n_x, n_y, CORES), ("parts", "uly", "y", "core"))
    swap = [(2 * x + c, 2 * x + 1 - c) for x in range(n_x) for c in range(CORES)]
    ring = [
        (2 * x + c, 2 * ((x + 1 - 2 * c) % n_x) + c) for x in range(n_x) for c in range(CORES)
    ]

    def on_device(queries, keys, values, doc_blocks):
        chunk = queries.shape[1]
        wide = queries.shape[2] // n_y
        mine = lax.all_to_all(by_head(keys, values, n_y), "y", 0, 0, tiled=True)
        q = jnp.transpose(queries[0].reshape(chunk, n_y, wide), (1, 0, 2))
        q = lax.all_to_all(q, "y", 0, 0, tiled=True)

        def step(a):
            return lax.ppermute(a, ("uly", "core"), ring)

        def other_core(a):
            return lax.ppermute(a, ("uly", "core"), swap)

        other = other_core(mine)
        pieces = [(mine, 0, 0), (other, 0, 1)]
        m, o = mine, other
        for k in range(1, n_x // 2 + 1):
            m = step(m)
            pieces += [(m, k, 0), (other_core(m), -k, 1)]
            if k < n_x // 2:
                o = step(o)
                pieces += [(o, k, 1), (other_core(o), -k, 0)]
        heads = attention(doc_blocks, q, pieces)
        back = lax.all_to_all(heads, "y", 0, 0, tiled=True)
        return side_by_side(back)

    return jax.shard_map(
        on_device,
        mesh=fine,
        in_specs=(
            P(("parts", "y", "core"), "uly", None),
            P(("parts", "y", "core"), "uly", None),
            P(("parts", "y", "core"), "uly", None),
            P("parts"),
        ),
        out_specs=P(("parts", "y", "core"), "uly", None),
        check_vma=False,
    )
```

time: 133 us -> 127 us (0.955)
  the two profiles are of different devices: /device:TPU:513 before, /device:TPU:528 now
where the time goes in v2:
time: 127 us; the launch traced here: 126 us
  waiting for transfers between devices  35.8 us (28%)
  blocking collectives  30.5 us (24%)
  starting transfers between devices  28.7 us (23%)
  Pallas kernels  27.1 us (21%)
  local copies, waits for them, and re-layouts  3.85 us (3%)
    all_to_all x1, blocking collectives, on_device(): back = lax.all_to_all(heads, 'y', 0, 0, tiled=True)  30.5 us
    ppermute x7, waiting for transfers between devices, step(): return lax.ppermute(a, ('uly', 'core'), ring)  27.7 us
    pallas_call x1, Pallas kernels, attention(): pl.pallas_call(kernel, in_specs=[smem, vmem] + [hbm] * (n - LATE) + [vmem...  24.3 us
    all_to_all x1, starting transfers between devices, on_device(): mine = lax.all_to_all(by_head(keys, values, n_y), 'y', 0, 0, tiled=True)  21.6 us
    all_to_all x1, waiting for transfers between devices, on_device(): mine = lax.all_to_all(by_head(keys, values, n_y), 'y', 0, 0, tiled=True)  6.71 us
    all_to_all x1, starting transfers between devices, on_device(): q = lax.all_to_all(q, 'y', 0, 0, tiled=True)  5.85 us
  transfers between devices with their start and end apart: 17, of which 9 were waited for; matrix products, arithmetic and copies ran while one was open for 2% of the time, Pallas kernels for 0%

profile of v2, /device:TPU:528, one launch (start us, length us, event | category | flops | bytes accessed | tf_op | source)
XLA Modules:
  0.0 126.3 jit_solution(10845691383823759632)
XLA Ops:
  0.0 1.8 %shard_map.46 = bf16[8,2,64,128]{3,2,1,0:T(8,128)(2,1)} custom-call(bf16[1,64,1024]{2,1,0:T(8,128)(2,1)} %k_ref.1, bf16[1,64,1024]{2,1,0:T(8,128)(2,1)} %v_ref.1), custom_call_target="tpu_custom_call" | custom-call | tf_op jit(solution)/shard_map/pallas_call | solution.py:151
  1.8 21.6 %all-to-all-start.1 = ((bf16[8,2,64,128]{3,2,1,0:T(8,128)(2,1)}), bf16[8,2,64,128]{3,2,1,0:T(8,128)(2,1)S(1)}, u32[]{:S(2)}, u32[]{:S(2)}) async-start(bf16[8,2,64,128]{3,2,1,0:T(8,128)(2,1)} %shard_map.46), calls=%async_computation.1 | async-start | bytes 524288 | tf_op jit(solution)/shard_map/all_to_all | solution.py:193
  23.4 0.6 copy.6
  24.0 1.5 %copy.8 = bf16[64,8,1024]{2,0,1:T(8,128)(2,1)} copy(bf16[64,8,1024]{2,1,0:T(8,128)(2,1)S(1)} %bitcast.6) | data formatting | bytes 2097152 | tf_op jit(solution)/shard_map/reshape;squeeze | solution.py:194
  25.5 6.7 %all-to-all-done.1.refs_0_ = bf16[8,2,64,128]{3,2,1,0:T(8,128)(2,1)S(1)} async-done(((bf16[8,2,64,128]{3,2,1,0:T(8,128)(2,1)}), bf16[8,2,64,128]{3,2,1,0:T(8,128)(2,1)S(1)}, u32[]{:S(2)}, u32[]{:S(2)}) %all-to-all-start.1) | async-done | bytes 262176 | tf_op jit(solution)/shard_map/all_to_all | solution.py:193
  32.2 5.9 %all-to-all-start = ((bf16[8,64,1024]{2,1,0:T(8,128)(2,1)}), bf16[8,64,1024]{2,1,0:T(8,128)(2,1)S(1)}, u32[]{:S(2)}, u32[]{:S(2)}) async-start(bf16[8,64,1024]{2,1,0:T(8,128)(2,1)} %bitcast.5), calls=%async_computation | async-start | bytes 2097152 | tf_op jit(solution)/shard_map/all_to_all | solution.py:195
  38.1 0.0 collective-permute-start
  38.1 0.0 copy-done.1
  38.1 0.1 collective-permute-start.1
  38.2 1.4 %collective-permute-done.refs_1_ = bf16[8,2,64,128]{3,2,1,0:T(8,128)(2,1)S(1)} collective-permute-done((bf16[8,2,64,128]{3,2,1,0:T(8,128)(2,1)S(1)}, bf16[8,2,64,128]{3,2,1,0:T(8,128)(2,1)S(1)}, u32[]{:S(2)}, u32[]{:S(2)}) %collective-permute-start) | collective-permute-done | bytes 262176 | tf_op jit(solution)/shard_map/ppermute | solution.py:201
  39.6 0.0 collective-permute-start.3
  39.6 6.2 %collective-permute-done.1.refs_2_ = bf16[8,2,64,128]{3,2,1,0:T(8,128)(2,1)S(1)} collective-permute-done((bf16[8,2,64,128]{3,2,1,0:T(8,128)(2,1)S(1)}, bf16[8,2,64,128]{3,2,1,0:T(8,128)(2,1)S(1)}, u32[]{:S(2)}, u32[]{:S(2)}) %collective-permute-start.1) | collective-permute-done | bytes 262176 | tf_op jit(solution)/shard_map/ppermute | solution.py:198
  45.8 0.0 collective-permute-start.5
  45.8 2.8 %collective-permute-done.3.refs_4_ = bf16[8,2,64,128]{3,2,1,0:T(8,128)(2,1)S(1)} collective-permute-done((bf16[8,2,64,128]{3,2,1,0:T(8,128)(2,1)S(1)}, bf16[8,2,64,128]{3,2,1,0:T(8,128)(2,1)S(1)}, u32[]{:S(2)}, u32[]{:S(2)}) %collective-permute-start.3) | collective-permute-done | bytes 262176 | tf_op jit(solution)/shard_map/ppermute | solution.py:198
  48.6 0.0 collective-permute-start.7
  48.6 4.8 %collective-permute-done.5.refs_6_ = bf16[8,2,64,128]{3,2,1,0:T(8,128)(2,1)S(1)} collective-permute-done((bf16[8,2,64,128]{3,2,1,0:T(8,128)(2,1)S(1)}, bf16[8,2,64,128]{3,2,1,0:T(8,128)(2,1)S(1)}, u32[]{:S(2)}, u32[]{:S(2)}) %collective-permute-start.5) | collective-permute-done | bytes 262176 | tf_op jit(solution)/shard_map/ppermute | solution.py:198
  53.4 0.0 collective-permute-start.9
  53.4 0.0 collective-permute-start.2
  53.4 0.5 collective-permute-start.4
  53.9 2.3 %collective-permute-done.7.refs_8_ = bf16[8,2,64,128]{3,2,1,0:T(8,128)(2,1)S(1)} collective-permute-done((bf16[8,2,64,128]{3,2,1,0:T(8,128)(2,1)S(1)}, bf16[8,2,64,128]{3,2,1,0:T(8,128)(2,1)S(1)}, u32[]{:S(2)}, u32[]{:S(2)}) %collective-permute-start.7) | collective-permute-done | bytes 262176 | tf_op jit(solution)/shard_map/ppermute | solution.py:198
  56.2 0.0 collective-permute-start.11
  56.2 4.8 %collective-permute-done.9.refs_10_ = bf16[8,2,64,128]{3,2,1,0:T(8,128)(2,1)S(1)} collective-permute-done((bf16[8,2,64,128]{3,2,1,0:T(8,128)(2,1)S(1)}, bf16[8,2,64,128]{3,2,1,0:T(8,128)(2,1)S(1)}, u32[]{:S(2)}, u32[]{:S(2)}) %collective-permute-start.9) | collective-permute-done | bytes 262176 | tf_op jit(solution)/shard_map/ppermute | solution.py:198
  61.0 0.0 collective-permute-start.13
  61.0 0.0 collective-permute-start.6
  61.0 0.0 collective-permute-done.2.refs_3_
  61.0 0.5 collective-permute-start.8
  61.5 0.0 collective-permute-done.4.refs_5_
  61.5 0.1 collective-permute-start.10
  61.6 2.1 %collective-permute-done.11.refs_12_ = bf16[8,2,64,128]{3,2,1,0:T(8,128)(2,1)S(1)} collective-permute-done((bf16[8,2,64,128]{3,2,1,0:T(8,128)(2,1)S(1)}, bf16[8,2,64,128]{3,2,1,0:T(8,128)(2,1)S(1)}, u32[]{:S(2)}, u32[]{:S(2)}) %collective-permute-start.11) | collective-permute-done | bytes 262176 | tf_op jit(solution)/shard_map/ppermute | solution.py:198
  63.8 0.0 collective-permute-start.12
  63.8 4.8 %collective-permute-done.13.refs_14_ = bf16[8,2,64,128]{3,2,1,0:T(8,128)(2,1)S(1)} collective-permute-done((bf16[8,2,64,128]{3,2,1,0:T(8,128)(2,1)S(1)}, bf16[8,2,64,128]{3,2,1,0:T(8,128)(2,1)S(1)}, u32[]{:S(2)}, u32[]{:S(2)}) %collective-permute-start.13) | collective-permute-done | bytes 262176 | tf_op jit(solution)/shard_map/ppermute | solution.py:198
  68.5 0.0 collective-permute-start.14
  68.5 0.0 collective-permute-done.6.refs_7_
  68.6 0.0 collective-permute-done.8.refs_9_
  68.6 0.0 copy-start.14
  68.6 0.0 collective-permute-done.10.refs_11_
  68.6 0.0 collective-permute-done.12.refs_13_
  68.6 0.6 copy-done.12
  69.2 0.1 copy-done.13
  69.3 0.1 copy-done.14
  69.4 0.1 copy-done.15
  69.6 0.7 copy-done.16
  70.3 0.0 collective-permute-done.14.refs_15_
  70.3 0.0 all-to-all-done.q_ref
  70.3 0.0 copy-done.4
  70.4 24.3 %shard_map.47 = bf16[8,64,1024]{2,1,0:T(8,128)(2,1)S(1)} custom-call(s32[16]{0:T(128)S(1)} %copy-done, bf16[8,64,1024]{2,1,0:T(8,128)(2,1)S(1)} %all-to-all-done.q_ref, bf16[8,2,64,128]{3,2,1,0:T(8,128)(2,1)} %copy-done.1, bf16[8,2,64,128]{3,2,1,0:T(8,128)(2,1)} %copy-done.3, bf16[8,2,64,128]{3,2,1,0:T(8,128)(2,1)} %copy-done.4, ...), custom_call_target="tpu_custom_call" | custom-call | tf_op jit(solution)/shard_map/pallas_call | solution.py:125
  94.7 30.5 %all_to_all.15.a_ref = bf16[8,64,1024]{2,1,0:T(8,128)(2,1)S(1)} all-to-all(bf16[8,64,1024]{2,1,0:T(8,128)(2,1)S(1)} %shard_map.47), channel_id=1, replica_groups=mesh['parts'=2,'uly'=8,'y'=8,'core'=2] {'y'}, dimensions={0} | all-to-all | bytes 2097152 | tf_op jit(solution)/shard_map/all_to_all | solution.py:213
  125.1 1.0 shard_map.48
  (26 shorter events, 0.0 us)
Async XLA Ops:
  0.0 23.4 %copy-start.2 = (bf16[1,64,8192]{2,1,0:T(8,128)(2,1)S(1)}, bf16[1,64,8192]{2,1,0:T(8,128)(2,1)}, u32[]{:S(2)}) copy-start(bf16[1,64,8192]{2,1,0:T(8,128)(2,1)} %param.4) | copy-start | bytes 3145732
  1.8 30.4 %all-to-all-start.1 = ((bf16[8,2,64,128]{3,2,1,0:T(8,128)(2,1)}), bf16[8,2,64,128]{3,2,1,0:T(8,128)(2,1)S(1)}, u32[]{:S(2)}, u32[]{:S(2)}) async-start(bf16[8,2,64,128]{3,2,1,0:T(8,128)(2,1)} %shard_map.46), calls=%async_computation.1 | async-start | bytes 524288 | tf_op jit(solution)/shard_map/all_to_all | solution.py:193
  32.2 5.9 %copy-start.1 = (bf16[8,2,64,128]{3,2,1,0:T(8,128)(2,1)}, bf16[8,2,64,128]{3,2,1,0:T(8,128)(2,1)S(1)}, u32[]{:S(2)}) copy-start(bf16[8,2,64,128]{3,2,1,0:T(8,128)(2,1)S(1)} %all-to-all-done.1.refs_0_) | copy-start | bytes 786436
  32.2 38.1 %copy-start = (s32[16]{0:T(128)S(1)}, s32[16]{0:T(128)}, u32[]{:S(2)}) copy-start(s32[16]{0:T(128)} %doc.1) | copy-start | bytes 196
  32.2 38.0 %all-to-all-start = ((bf16[8,64,1024]{2,1,0:T(8,128)(2,1)}), bf16[8,64,1024]{2,1,0:T(8,128)(2,1)S(1)}, u32[]{:S(2)}, u32[]{:S(2)}) async-start(bf16[8,64,1024]{2,1,0:T(8,128)(2,1)} %bitcast.5), calls=%async_computation | async-start | bytes 2097152 | tf_op jit(solution)/shard_map/all_to_all | solution.py:195
  38.1 1.5 %collective-permute-start = (bf16[8,2,64,128]{3,2,1,0:T(8,128)(2,1)S(1)}, bf16[8,2,64,128]{3,2,1,0:T(8,128)(2,1)S(1)}, u32[]{:S(2)}, u32[]{:S(2)}) collective-permute-start(bf16[8,2,64,128]{3,2,1,0:T(8,128)(2,1)S(1)} %all-to-all-done.1.refs_0_), channel_id=1, source_target_pairs={{0,1},{1,0},{16,17},{17,16},{32,33},{33,32},{48,49},{49,48},{64,65... | collective-permute-start | bytes 786440 | tf_op jit(solution)/shard_map/ppermute | solution.py:201
  38.1 7.7 %collective-permute-start.1 = (bf16[8,2,64,128]{3,2,1,0:T(8,128)(2,1)S(1)}, bf16[8,2,64,128]{3,2,1,0:T(8,128)(2,1)S(1)}, u32[]{:S(2)}, u32[]{:S(2)}) collective-permute-start(bf16[8,2,64,128]{3,2,1,0:T(8,128)(2,1)S(1)} %all-to-all-done.1.refs_0_), channel_id=1, source_target_pairs={{0,16},{1,113},{16,32},{17,1},{32,48},{33,17},{48,64},{49,33},{64,... | collective-permute-start | bytes 786440 | tf_op jit(solution)/shard_map/ppermute | solution.py:198
  39.6 30.7 %copy-start.3 = (bf16[8,2,64,128]{3,2,1,0:T(8,128)(2,1)}, bf16[8,2,64,128]{3,2,1,0:T(8,128)(2,1)S(1)}, u32[]{:S(2)}) copy-start(bf16[8,2,64,128]{3,2,1,0:T(8,128)(2,1)S(1)} %collective-permute-done.refs_1_) | copy-start | bytes 786436
  39.6 9.0 %collective-permute-start.3 = (bf16[8,2,64,128]{3,2,1,0:T(8,128)(2,1)S(1)}, bf16[8,2,64,128]{3,2,1,0:T(8,128)(2,1)S(1)}, u32[]{:S(2)}, u32[]{:S(2)}) collective-permute-start(bf16[8,2,64,128]{3,2,1,0:T(8,128)(2,1)S(1)} %collective-permute-done.refs_1_), channel_id=1, source_target_pairs={{0,16},{1,113},{16,32},{17,1},{32,48},{33,17},{48,64},{49,33},{64,... | collective-permute-start | bytes 786440 | tf_op jit(solution)/shard_map/ppermute | solution.py:198
  45.8 24.5 %copy-start.4 = (bf16[8,2,64,128]{3,2,1,0:T(8,128)(2,1)}, bf16[8,2,64,128]{3,2,1,0:T(8,128)(2,1)S(1)}, u32[]{:S(2)}) copy-start(bf16[8,2,64,128]{3,2,1,0:T(8,128)(2,1)S(1)} %collective-permute-done.1.refs_2_) | copy-start | bytes 786436
  45.8 7.6 %collective-permute-start.5 = (bf16[8,2,64,128]{3,2,1,0:T(8,128)(2,1)S(1)}, bf16[8,2,64,128]{3,2,1,0:T(8,128)(2,1)S(1)}, u32[]{:S(2)}, u32[]{:S(2)}) collective-permute-start(bf16[8,2,64,128]{3,2,1,0:T(8,128)(2,1)S(1)} %collective-permute-done.1.refs_2_), channel_id=1, source_target_pairs={{0,16},{1,113},{16,32},{17,1},{32,48},{33,17},{48,64},{49,33},{64,... | collective-permute-start | bytes 786440 | tf_op jit(solution)/shard_map/ppermute | solution.py:198
  48.6 21.7 %copy-start.5 = (bf16[8,2,64,128]{3,2,1,0:T(8,128)(2,1)}, bf16[8,2,64,128]{3,2,1,0:T(8,128)(2,1)S(1)}, u32[]{:S(2)}) copy-start(bf16[8,2,64,128]{3,2,1,0:T(8,128)(2,1)S(1)} %collective-permute-done.3.refs_4_) | copy-start | bytes 786436
  48.6 7.6 %collective-permute-start.7 = (bf16[8,2,64,128]{3,2,1,0:T(8,128)(2,1)S(1)}, bf16[8,2,64,128]{3,2,1,0:T(8,128)(2,1)S(1)}, u32[]{:S(2)}, u32[]{:S(2)}) collective-permute-start(bf16[8,2,64,128]{3,2,1,0:T(8,128)(2,1)S(1)} %collective-permute-done.3.refs_4_), channel_id=1, source_target_pairs={{0,16},{1,113},{16,32},{17,1},{32,48},{33,17},{48,64},{49,33},{64,... | collective-permute-start | bytes 786440 | tf_op jit(solution)/shard_map/ppermute | solution.py:198
  53.4 16.9 %copy-start.6 = (bf16[8,2,64,128]{3,2,1,0:T(8,128)(2,1)}, bf16[8,2,64,128]{3,2,1,0:T(8,128)(2,1)S(1)}, u32[]{:S(2)}) copy-start(bf16[8,2,64,128]{3,2,1,0:T(8,128)(2,1)S(1)} %collective-permute-done.5.refs_6_) | copy-start | bytes 786436
  53.4 7.6 %collective-permute-start.9 = (bf16[8,2,64,128]{3,2,1,0:T(8,128)(2,1)S(1)}, bf16[8,2,64,128]{3,2,1,0:T(8,128)(2,1)S(1)}, u32[]{:S(2)}, u32[]{:S(2)}) collective-permute-start(bf16[8,2,64,128]{3,2,1,0:T(8,128)(2,1)S(1)} %collective-permute-done.5.refs_6_), channel_id=1, source_target_pairs={{0,16},{1,113},{16,32},{17,1},{32,48},{33,17},{48,64},{49,33},{64,... | collective-permute-start | bytes 786440 | tf_op jit(solution)/shard_map/ppermute | solution.py:198
  53.4 7.6 %collective-permute-start.2 = (bf16[8,2,64,128]{3,2,1,0:T(8,128)(2,1)S(1)}, bf16[8,2,64,128]{3,2,1,0:T(8,128)(2,1)S(1)}, u32[]{:S(2)}, u32[]{:S(2)}) collective-permute-start(bf16[8,2,64,128]{3,2,1,0:T(8,128)(2,1)S(1)} %collective-permute-done.1.refs_2_), channel_id=1, source_target_pairs={{0,1},{1,0},{16,17},{17,16},{32,33},{33,32},{48,49},{49,48},{64,65... | collective-permute-start | bytes 786440 | tf_op jit(solution)/shard_map/ppermute | solution.py:201
  53.4 8.1 %collective-permute-start.4 = (bf16[8,2,64,128]{3,2,1,0:T(8,128)(2,1)S(1)}, bf16[8,2,64,128]{3,2,1,0:T(8,128)(2,1)S(1)}, u32[]{:S(2)}, u32[]{:S(2)}) collective-permute-start(bf16[8,2,64,128]{3,2,1,0:T(8,128)(2,1)S(1)} %collective-permute-done.3.refs_4_), channel_id=1, source_target_pairs={{0,1},{1,0},{16,17},{17,16},{32,33},{33,32},{48,49},{49,48},{64,65... | collective-permute-start | bytes 786440 | tf_op jit(solution)/shard_map/ppermute | solution.py:201
  56.2 14.1 %copy-start.7 = (bf16[8,2,64,128]{3,2,1,0:T(8,128)(2,1)}, bf16[8,2,64,128]{3,2,1,0:T(8,128)(2,1)S(1)}, u32[]{:S(2)}) copy-start(bf16[8,2,64,128]{3,2,1,0:T(8,128)(2,1)S(1)} %collective-permute-done.7.refs_8_) | copy-start | bytes 786436
  56.2 7.6 %collective-permute-start.11 = (bf16[8,2,64,128]{3,2,1,0:T(8,128)(2,1)S(1)}, bf16[8,2,64,128]{3,2,1,0:T(8,128)(2,1)S(1)}, u32[]{:S(2)}, u32[]{:S(2)}) collective-permute-start(bf16[8,2,64,128]{3,2,1,0:T(8,128)(2,1)S(1)} %collective-permute-done.7.refs_8_), channel_id=1, source_target_pairs={{0,16},{1,113},{16,32},{17,1},{32,48},{33,17},{48,64},{49,33},{64,... | collective-permute-start | bytes 786440 | tf_op jit(solution)/shard_map/ppermute | solution.py:198
  61.0 9.4 %copy-start.8 = (bf16[8,2,64,128]{3,2,1,0:T(8,128)(2,1)}, bf16[8,2,64,128]{3,2,1,0:T(8,128)(2,1)S(1)}, u32[]{:S(2)}) copy-start(bf16[8,2,64,128]{3,2,1,0:T(8,128)(2,1)S(1)} %collective-permute-done.9.refs_10_) | copy-start | bytes 786436
  61.0 7.6 %collective-permute-start.13 = (bf16[8,2,64,128]{3,2,1,0:T(8,128)(2,1)S(1)}, bf16[8,2,64,128]{3,2,1,0:T(8,128)(2,1)S(1)}, u32[]{:S(2)}, u32[]{:S(2)}) collective-permute-start(bf16[8,2,64,128]{3,2,1,0:T(8,128)(2,1)S(1)} %collective-permute-done.9.refs_10_), channel_id=1, source_target_pairs={{0,16},{1,113},{16,32},{17,1},{32,48},{33,17},{48,64},{49,33},{64,... | collective-permute-start | bytes 786440 | tf_op jit(solution)/shard_map/ppermute | solution.py:198
  61.0 7.6 %collective-permute-start.6 = (bf16[8,2,64,128]{3,2,1,0:T(8,128)(2,1)S(1)}, bf16[8,2,64,128]{3,2,1,0:T(8,128)(2,1)S(1)}, u32[]{:S(2)}, u32[]{:S(2)}) collective-permute-start(bf16[8,2,64,128]{3,2,1,0:T(8,128)(2,1)S(1)} %collective-permute-done.5.refs_6_), channel_id=1, source_target_pairs={{0,1},{1,0},{16,17},{17,16},{32,33},{33,32},{48,49},{49,48},{64,65... | collective-permute-start | bytes 786440 | tf_op jit(solution)/shard_map/ppermute | solution.py:201
  61.0 9.4 %copy-start.9 = (bf16[8,2,64,128]{3,2,1,0:T(8,128)(2,1)}, bf16[8,2,64,128]{3,2,1,0:T(8,128)(2,1)S(1)}, u32[]{:S(2)}) copy-start(bf16[8,2,64,128]{3,2,1,0:T(8,128)(2,1)S(1)} %collective-permute-done.2.refs_3_) | copy-start | bytes 786436
  61.0 7.6 %collective-permute-start.8 = (bf16[8,2,64,128]{3,2,1,0:T(8,128)(2,1)S(1)}, bf16[8,2,64,128]{3,2,1,0:T(8,128)(2,1)S(1)}, u32[]{:S(2)}, u32[]{:S(2)}) collective-permute-start(bf16[8,2,64,128]{3,2,1,0:T(8,128)(2,1)S(1)} %collective-permute-done.7.refs_8_), channel_id=1, source_target_pairs={{0,1},{1,0},{16,17},{17,16},{32,33},{33,32},{48,49},{49,48},{64,65... | collective-permute-start | bytes 786440 | tf_op jit(solution)/shard_map/ppermute | solution.py:201
  61.5 8.9 %copy-start.10 = (bf16[8,2,64,128]{3,2,1,0:T(8,128)(2,1)}, bf16[8,2,64,128]{3,2,1,0:T(8,128)(2,1)S(1)}, u32[]{:S(2)}) copy-start(bf16[8,2,64,128]{3,2,1,0:T(8,128)(2,1)S(1)} %collective-permute-done.4.refs_5_) | copy-start | bytes 786436
  61.5 7.1 %collective-permute-start.10 = (bf16[8,2,64,128]{3,2,1,0:T(8,128)(2,1)S(1)}, bf16[8,2,64,128]{3,2,1,0:T(8,128)(2,1)S(1)}, u32[]{:S(2)}, u32[]{:S(2)}) collective-permute-start(bf16[8,2,64,128]{3,2,1,0:T(8,128)(2,1)S(1)} %collective-permute-done.9.refs_10_), channel_id=1, source_target_pairs={{0,1},{1,0},{16,17},{17,16},{32,33},{33,32},{48,49},{49,48},{64,65... | collective-permute-start | bytes 786440 | tf_op jit(solution)/shard_map/ppermute | solution.py:201
  63.8 6.6 %copy-start.11 = (bf16[8,2,64,128]{3,2,1,0:T(8,128)(2,1)}, bf16[8,2,64,128]{3,2,1,0:T(8,128)(2,1)S(1)}, u32[]{:S(2)}) copy-start(bf16[8,2,64,128]{3,2,1,0:T(8,128)(2,1)S(1)} %collective-permute-done.11.refs_12_) | copy-start | bytes 786436
  63.8 4.8 %collective-permute-start.12 = (bf16[8,2,64,128]{3,2,1,0:T(8,128)(2,1)S(1)}, bf16[8,2,64,128]{3,2,1,0:T(8,128)(2,1)S(1)}, u32[]{:S(2)}, u32[]{:S(2)}) collective-permute-start(bf16[8,2,64,128]{3,2,1,0:T(8,128)(2,1)S(1)} %collective-permute-done.11.refs_12_), channel_id=1, source_target_pairs={{0,1},{1,0},{16,17},{17,16},{32,33},{33,32},{48,49},{49,48},{64,65... | collective-permute-start | bytes 786440 | tf_op jit(solution)/shard_map/ppermute | solution.py:201
  68.5 0.7 copy-start.12
  68.5 1.7 %collective-permute-start.14 = (bf16[8,2,64,128]{3,2,1,0:T(8,128)(2,1)S(1)}, bf16[8,2,64,128]{3,2,1,0:T(8,128)(2,1)}, u32[]{:S(2)}, u32[]{:S(2)}) collective-permute-start(bf16[8,2,64,128]{3,2,1,0:T(8,128)(2,1)S(1)} %collective-permute-done.13.refs_14_), channel_id=1, source_target_pairs={{0,1},{1,0},{16,17},{17,16},{32,33},{33,32},{48,49},{49,48},{64,65... | collective-permute-start | bytes 786440 | tf_op jit(solution)/shard_map/ppermute | solution.py:201
  68.5 0.8 copy-start.13
  68.6 0.9 copy-start.14
  68.6 1.0 copy-start.15
  69.6 0.7 copy-start.16

commit v3 on v2

v3 whole, which is shorter than its diff:
```python
import jax
import jax.numpy as jnp
from jax import lax
from jax.experimental import pallas as pl
from jax.experimental.pallas import tpu as pltpu
from jax.sharding import Mesh, PartitionSpec as P


HEAD_WIDTH = 128
BLOCK = 128
CORES = 2
EXTRA = 16
VMEM_LIMIT = 32 << 20
LOG2E = 1.4426950408889634
SCALE = LOG2E * HEAD_WIDTH ** -0.5


def in_vmem(a):
    return pltpu.with_memory_space_constraint(a, pltpu.VMEM)


def in_hbm(a):
    return pltpu.with_memory_space_constraint(a, pltpu.HBM)


def attention(docs, q, pieces):
    blocks, chunk, wide = q.shape
    heads = wide // HEAD_WIDTH
    rows = heads * chunk
    arrays = [p[0] for p in pieces]
    n = len(arrays)
    n_x = n // CORES
    tile = n_x * chunk
    n_docs = docs.shape[0]

    def kernel(doc, q_ref, *refs):
        srcs, (o_ref, kv, q_t, p_buf, a_ref, m_ref, bad_ref, sems) = refs[:n], refs[n:]
        x = lax.axis_index("uly")
        core = lax.axis_index("core")
        way = 1 - 2 * core
        copies = [
            pltpu.make_async_copy(
                srcs[i],
                kv.at[core + pieces[i][2] * way, (x - way * pieces[i][1]) % n_x],
                sems.at[i],
            )
            for i in range(n)
        ]
        for c in copies:
            c.start()
        bad_ref[...] = jnp.zeros_like(bad_ref)
        ones = jnp.ones((EXTRA, tile), jnp.bfloat16)

        def load(j, kind):
            return jnp.concatenate(
                [kv[lax.rem(j, CORES), a, lax.div(j, CORES), kind] for a in range(n_x)], axis=0
            )

        def span(step):
            last = step * CORES + core
            first = last * tile + x * chunk
            begin = jnp.int32(0)
            end = jnp.int32(0)
            for i in range(n_docs):
                end = end + doc[i] * BLOCK
                begin = jnp.where(end <= first, end, begin)
            return last, first, begin, lax.div(begin, tile)

        def prepare(step):
            qs = jnp.concatenate(
                [q_ref[step, :, h * HEAD_WIDTH : (h + 1) * HEAD_WIDTH] for h in range(heads)], axis=0
            )
            qf = jnp.transpose(qs.astype(jnp.float32) * SCALE)
            high = qf.astype(jnp.bfloat16)
            q_t[step & 1, :HEAD_WIDTH] = high
            q_t[step & 1, HEAD_WIDTH:] = (qf - high.astype(jnp.float32)).astype(jnp.bfloat16)

        def scores(step, j):
            kt = load(j, 0)
            return jnp.dot(
                jnp.concatenate([kt, kt], axis=1), q_t[step & 1], preferred_element_type=jnp.float32
            )

        def values(j, begin):
            vt = jnp.concatenate([jnp.transpose(load(j, 1)), ones], axis=0)
            at = lax.broadcasted_iota(jnp.int32, (1, tile), 1) + j * tile
            return vt * (at >= begin).astype(jnp.float32).astype(jnp.bfloat16)

        def allowed(j, first, begin):
            key = lax.broadcasted_iota(jnp.int32, (tile, rows), 0) + j * tile
            row = (lax.broadcasted_iota(jnp.int32, (tile, rows), 1) & (chunk - 1)) + first
            return (key <= row) & (key >= begin)

        def finish(step):
            out = a_ref[:HEAD_WIDTH] * (1.0 / a_ref[HEAD_WIDTH : HEAD_WIDTH + 1])
            out = jnp.transpose(out).astype(jnp.bfloat16)
            for h in range(heads):
                o_ref[step, :, h * HEAD_WIDTH : (h + 1) * HEAD_WIDTH] = out[
                    h * chunk : (h + 1) * chunk
                ]

        prepare(0)
        for c in copies:
            c.wait()

        @pl.loop(0, blocks)
        def _(step):
            last, first, begin, lowest = span(step)
            s = jnp.where(allowed(last, first, begin), scores(step, last), -1e30)
            top = jnp.max(s, axis=0, keepdims=True)
            m_ref[:1] = top
            p_buf[0] = jnp.exp2(s - top).astype(jnp.bfloat16)
            a_ref[...] = jnp.zeros_like(a_ref)

            def weights(j):
                return jnp.exp2(scores(step, j) - m_ref[:1]).astype(jnp.bfloat16)

            def product(j, slot):
                return jnp.dot(
                    values(j, begin), p_buf[slot], preferred_element_type=jnp.float32
                )

            count = last - lowest

            @pl.loop(0, lax.div(count, 2))
            def _(h):
                j = last - 2 * h
                p1 = weights(j - 1)
                a0 = product(j, 0)
                p2 = weights(j - 2)
                p_buf[1] = p1
                a1 = product(j - 1, 1)
                a_ref[...] += a0 + a1
                p_buf[0] = p2

            @pl.when(lax.rem(count, 2) == 1)
            def _():
                p1 = weights(lowest)
                a_ref[...] += product(lowest + 1, 0)
                p_buf[0] = p1

            a_ref[...] += product(lowest, 0)
            total = a_ref[HEAD_WIDTH : HEAD_WIDTH + 1]
            bad_ref[:1] = jnp.maximum(bad_ref[:1], jnp.where(total < 1e30, 0.0, 1.0))
            prepare(jnp.minimum(step + 1, blocks - 1))
            finish(step)

        @pl.when(jnp.max(bad_ref[...]) > 0.0)
        def _():
            @pl.loop(0, blocks)
            def _(step):
                last, first, begin, lowest = span(step)
                prepare(step)
                m_ref[...] = jnp.full_like(m_ref, -1e30)
                a_ref[...] = jnp.zeros_like(a_ref)

                @pl.loop(lowest, last + 1)
                def _(j):
                    s = jnp.where(allowed(j, first, begin), scores(step, j), -1e30)
                    old = m_ref[:1]
                    top = jnp.maximum(old, jnp.max(s, axis=0, keepdims=True))
                    m_ref[:1] = top
                    p = jnp.exp2(s - top).astype(jnp.bfloat16)
                    a_ref[...] = a_ref[...] * jnp.exp2(old - top) + jnp.dot(
                        values(j, begin), p, preferred_element_type=jnp.float32
                    )

                finish(step)

    smem = pl.BlockSpec(memory_space=pltpu.SMEM)
    hbm = pl.BlockSpec(memory_space=pltpu.HBM)
    vmem = pl.BlockSpec(memory_space=pltpu.VMEM)
    return pl.pallas_call(
        kernel,
        in_specs=[smem, vmem] + [hbm] * n,
        out_specs=vmem,
        out_shape=pltpu.VMEM(q.shape, jnp.bfloat16),
        scratch_shapes=[
            pltpu.VMEM((CORES, n_x, blocks, 2, chunk, HEAD_WIDTH), jnp.bfloat16),
            pltpu.VMEM((2, 2 * HEAD_WIDTH, rows), jnp.bfloat16),
            pltpu.VMEM((2, tile, rows), jnp.bfloat16),
            pltpu.VMEM((HEAD_WIDTH + EXTRA, rows), jnp.float32),
            pltpu.VMEM((8, rows), jnp.float32),
            pltpu.VMEM((8, rows), jnp.float32),
            pltpu.SemaphoreType.DMA((n,)),
        ],
        compiler_params=pltpu.CompilerParams(vmem_limit_bytes=VMEM_LIMIT),
    )(docs, in_vmem(q), *[in_hbm(a) for a in arrays])


def by_head(keys, values, heads):
    chunk = keys.shape[1]

    def kernel(k_ref, v_ref, o_ref):
        for h in range(heads):
            o_ref[h, 0] = k_ref[0, :, h * HEAD_WIDTH : (h + 1) * HEAD_WIDTH]
            o_ref[h, 1] = v_ref[0, :, h * HEAD_WIDTH : (h + 1) * HEAD_WIDTH]

    vmem = pl.BlockSpec(memory_space=pltpu.VMEM)
    return pl.pallas_call(
        kernel,
        in_specs=[vmem, vmem],
        out_specs=vmem,
        out_shape=pltpu.VMEM((heads, 2, chunk, HEAD_WIDTH), keys.dtype),
    )(keys, values)


def side_by_side(a):
    groups, chunk, wide = a.shape

    def kernel(a_ref, o_ref, sems):
        copies = [
            pltpu.make_async_copy(a_ref.at[g], o_ref.at[0, :, pl.ds(g * wide, wide)], sems.at[g])
            for g in range(groups)
        ]
        for c in copies:
            c.start()
        for c in copies:
            c.wait()

    return pl.pallas_call(
        kernel,
        in_specs=[pl.BlockSpec(memory_space=pltpu.VMEM)],
        out_specs=pl.BlockSpec(memory_space=pltpu.HBM),
        out_shape=jax.ShapeDtypeStruct((1, chunk, groups * wide), a.dtype),
        scratch_shapes=[pltpu.SemaphoreType.DMA((groups,))],
    )(in_vmem(a))


def solution(mesh):
    parts, n_x, blk = mesh.devices.shape
    n_y = blk // CORES
    fine = Mesh(mesh.devices.reshape(parts, n_x, n_y, CORES), ("parts", "uly", "y", "core"))
    swap = [(2 * x + c, 2 * x + 1 - c) for x in range(n_x) for c in range(CORES)]
    ring = [
        (2 * x + c, 2 * ((x + 1 - 2 * c) % n_x) + c) for x in range(n_x) for c in range(CORES)
    ]

    def on_device(queries, keys, values, doc_blocks):
        chunk = queries.shape[1]
        wide = queries.shape[2] // n_y
        mine = lax.all_to_all(by_head(keys, values, n_y), "y", 0, 0, tiled=True)
        q = jnp.transpose(queries[0].reshape(chunk, n_y, wide), (1, 0, 2))
        q = lax.all_to_all(q, "y", 0, 0, tiled=True)

        def step(a):
            return lax.ppermute(a, ("uly", "core"), ring)

        def other_core(a):
            return lax.ppermute(a, ("uly", "core"), swap)

        other = other_core(mine)
        pieces = [(mine, 0, 0), (other, 0, 1)]
        m, o = mine, other
        for k in range(1, n_x // 2 + 1):
            m = step(m)
            pieces += [(m, k, 0), (other_core(m), -k, 1)]
            if k < n_x // 2:
                o = step(o)
                pieces += [(o, k, 1), (other_core(o), -k, 0)]
        heads = attention(doc_blocks, q, pieces)
        back = lax.all_to_all(heads, "y", 0, 0, tiled=True)
        return side_by_side(back)

    return jax.shard_map(
        on_device,
        mesh=fine,
        in_specs=(
            P(("parts", "y", "core"), "uly", None),
            P(("parts", "y", "core"), "uly", None),
            P(("parts", "y", "core"), "uly", None),
            P("parts"),
        ),
        out_specs=P(("parts", "y", "core"), "uly", None),
        check_vma=False,
    )
```

time: 127 us -> 125 us (0.984)
  the two profiles are of different devices: /device:TPU:528 before, /device:TPU:513 now
where the time goes in v3:
time: 125 us
  starting transfers between devices  51.3 us (41%)
  blocking collectives  33.5 us (27%)
  Pallas kernels  20.1 us (16%)
  waiting for transfers between devices  15.9 us (13%)
  local copies, waits for them, and re-layouts  3.77 us (3%)
    all_to_all x1, blocking collectives, on_device(): back = lax.all_to_all(heads, 'y', 0, 0, tiled=True)  33.5 us
    ppermute x8, starting transfers between devices, other_core(): return lax.ppermute(a, ('uly', 'core'), swap)  24.2 us
    pallas_call x1, Pallas kernels, attention(): pl.pallas_call(kernel, in_specs=[smem, vmem] + [hbm] * n, out_specs=vmem,...  17.3 us
    all_to_all x1, starting transfers between devices, on_device(): mine = lax.all_to_all(by_head(keys, values, n_y), 'y', 0, 0, tiled=True)  13.7 us
    ppermute x7, starting transfers between devices, step(): return lax.ppermute(a, ('uly', 'core'), ring)  9.49 us
    ppermute x7, waiting for transfers between devices, step(): return lax.ppermute(a, ('uly', 'core'), ring)  7.55 us
    all_to_all x1, waiting for transfers between devices, on_device(): mine = lax.all_to_all(by_head(keys, values, n_y), 'y', 0, 0, tiled=True)  7.17 us
    all_to_all x1, starting transfers between devices, on_device(): q = lax.all_to_all(q, 'y', 0, 0, tiled=True)  3.9 us
  transfers between devices with their start and end apart: 17, of which 5 were waited for; matrix products, arithmetic and copies ran while one was open for 2% of the time, Pallas kernels for 0%

profile of v3, /device:TPU:513, one launch (start us, length us, event | category | flops | bytes accessed | tf_op | source)
XLA Modules:
  0.0 124.8 jit_solution(3828670903233456201)
XLA Ops:
  0.0 1.8 %shard_map.46 = bf16[8,2,64,128]{3,2,1,0:T(8,128)(2,1)} custom-call(bf16[1,64,1024]{2,1,0:T(8,128)(2,1)} %k_ref.1, bf16[1,64,1024]{2,1,0:T(8,128)(2,1)} %v_ref.1), custom_call_target="tpu_custom_call" | custom-call | tf_op jit(solution)/shard_map/pallas_call | solution.py:200
  1.8 13.7 %all-to-all-start.1 = ((bf16[8,2,64,128]{3,2,1,0:T(8,128)(2,1)}), bf16[8,2,64,128]{3,2,1,0:T(8,128)(2,1)S(1)}, u32[]{:S(2)}, u32[]{:S(2)}) async-start(bf16[8,2,64,128]{3,2,1,0:T(8,128)(2,1)} %shard_map.46), calls=%async_computation.1 | async-start | bytes 524288 | tf_op jit(solution)/shard_map/all_to_all | solution.py:242
  15.5 0.6 copy.6
  16.1 1.5 %copy.8 = bf16[64,8,1024]{2,0,1:T(8,128)(2,1)} copy(bf16[64,8,1024]{2,1,0:T(8,128)(2,1)S(1)} %bitcast.6) | data formatting | bytes 2097152 | tf_op jit(solution)/shard_map/reshape;squeeze | solution.py:243
  17.7 7.2 %all-to-all-done.1.refs_0_ = bf16[8,2,64,128]{3,2,1,0:T(8,128)(2,1)S(1)} async-done(((bf16[8,2,64,128]{3,2,1,0:T(8,128)(2,1)}), bf16[8,2,64,128]{3,2,1,0:T(8,128)(2,1)S(1)}, u32[]{:S(2)}, u32[]{:S(2)}) %all-to-all-start.1) | async-done | bytes 262176 | tf_op jit(solution)/shard_map/all_to_all | solution.py:242
  24.8 3.9 %all-to-all-start = ((bf16[8,64,1024]{2,1,0:T(8,128)(2,1)}), bf16[8,64,1024]{2,1,0:T(8,128)(2,1)S(1)}, u32[]{:S(2)}, u32[]{:S(2)}) async-start(bf16[8,64,1024]{2,1,0:T(8,128)(2,1)} %bitcast.5), calls=%async_computation | async-start | bytes 2097152 | tf_op jit(solution)/shard_map/all_to_all | solution.py:244
  28.7 11.9 %collective-permute-start = (bf16[8,2,64,128]{3,2,1,0:T(8,128)(2,1)S(1)}, bf16[8,2,64,128]{3,2,1,0:T(8,128)(2,1)S(1)}, u32[]{:S(2)}, u32[]{:S(2)}) collective-permute-start(bf16[8,2,64,128]{3,2,1,0:T(8,128)(2,1)S(1)} %all-to-all-done.1.refs_0_), channel_id=1, source_target_pairs={{0,1},{1,0},{16,17},{17,16},{32,33},{33,32},{48,49},{49,48},{64,65... | collective-permute-start | bytes 786440 | tf_op jit(solution)/shard_map/ppermute | solution.py:250
  40.7 0.0 collective-permute-start.1
  40.7 1.2 collective-permute-done.refs_1_
  41.8 0.0 collective-permute-start.3
  41.8 4.4 %collective-permute-done.1.refs_2_ = bf16[8,2,64,128]{3,2,1,0:T(8,128)(2,1)S(1)} collective-permute-done((bf16[8,2,64,128]{3,2,1,0:T(8,128)(2,1)S(1)}, bf16[8,2,64,128]{3,2,1,0:T(8,128)(2,1)S(1)}, u32[]{:S(2)}, u32[]{:S(2)}) %collective-permute-start.1) | collective-permute-done | bytes 262176 | tf_op jit(solution)/shard_map/ppermute | solution.py:247
  46.2 1.2 collective-permute-start.5
  47.4 1.6 %collective-permute-done.3.refs_4_ = bf16[8,2,64,128]{3,2,1,0:T(8,128)(2,1)S(1)} collective-permute-done((bf16[8,2,64,128]{3,2,1,0:T(8,128)(2,1)S(1)}, bf16[8,2,64,128]{3,2,1,0:T(8,128)(2,1)S(1)}, u32[]{:S(2)}, u32[]{:S(2)}) %collective-permute-start.3) | collective-permute-done | bytes 262176 | tf_op jit(solution)/shard_map/ppermute | solution.py:247
  49.0 1.2 collective-permute-start.7
  50.2 1.6 %collective-permute-done.5.refs_6_ = bf16[8,2,64,128]{3,2,1,0:T(8,128)(2,1)S(1)} collective-permute-done((bf16[8,2,64,128]{3,2,1,0:T(8,128)(2,1)S(1)}, bf16[8,2,64,128]{3,2,1,0:T(8,128)(2,1)S(1)}, u32[]{:S(2)}, u32[]{:S(2)}) %collective-permute-start.5) | collective-permute-done | bytes 262176 | tf_op jit(solution)/shard_map/ppermute | solution.py:247
  51.8 2.3 %collective-permute-start.9 = (bf16[8,2,64,128]{3,2,1,0:T(8,128)(2,1)S(1)}, bf16[8,2,64,128]{3,2,1,0:T(8,128)(2,1)S(1)}, u32[]{:S(2)}, u32[]{:S(2)}) collective-permute-start(bf16[8,2,64,128]{3,2,1,0:T(8,128)(2,1)S(1)} %collective-permute-done.5.refs_6_), channel_id=1, source_target_pairs={{0,16},{1,113},{16,32},{17,1},{32,48},{33,17},{48,64},{49,33},{64,... | collective-permute-start | bytes 786440 | tf_op jit(solution)/shard_map/ppermute | solution.py:247
  54.1 1.9 %collective-permute-start.2 = (bf16[8,2,64,128]{3,2,1,0:T(8,128)(2,1)S(1)}, bf16[8,2,64,128]{3,2,1,0:T(8,128)(2,1)S(1)}, u32[]{:S(2)}, u32[]{:S(2)}) collective-permute-start(bf16[8,2,64,128]{3,2,1,0:T(8,128)(2,1)S(1)} %collective-permute-done.1.refs_2_), channel_id=1, source_target_pairs={{0,1},{1,0},{16,17},{17,16},{32,33},{33,32},{48,49},{49,48},{64,65... | collective-permute-start | bytes 786440 | tf_op jit(solution)/shard_map/ppermute | solution.py:250
  56.0 0.1 collective-permute-start.4
  56.1 0.0 collective-permute-done.7.refs_8_
  56.1 2.9 %collective-permute-start.11 = (bf16[8,2,64,128]{3,2,1,0:T(8,128)(2,1)S(1)}, bf16[8,2,64,128]{3,2,1,0:T(8,128)(2,1)S(1)}, u32[]{:S(2)}, u32[]{:S(2)}) collective-permute-start(bf16[8,2,64,128]{3,2,1,0:T(8,128)(2,1)S(1)} %collective-permute-done.7.refs_8_), channel_id=1, source_target_pairs={{0,16},{1,113},{16,32},{17,1},{32,48},{33,17},{48,64},{49,33},{64,... | collective-permute-start | bytes 786440 | tf_op jit(solution)/shard_map/ppermute | solution.py:247
  59.1 0.0 collective-permute-done.9.refs_10_
  59.1 1.8 %collective-permute-start.13 = (bf16[8,2,64,128]{3,2,1,0:T(8,128)(2,1)S(1)}, bf16[8,2,64,128]{3,2,1,0:T(8,128)(2,1)S(1)}, u32[]{:S(2)}, u32[]{:S(2)}) collective-permute-start(bf16[8,2,64,128]{3,2,1,0:T(8,128)(2,1)S(1)} %collective-permute-done.9.refs_10_), channel_id=1, source_target_pairs={{0,16},{1,113},{16,32},{17,1},{32,48},{33,17},{48,64},{49,33},{64,... | collective-permute-start | bytes 786440 | tf_op jit(solution)/shard_map/ppermute | solution.py:247
  60.9 2.7 %collective-permute-start.6 = (bf16[8,2,64,128]{3,2,1,0:T(8,128)(2,1)S(1)}, bf16[8,2,64,128]{3,2,1,0:T(8,128)(2,1)S(1)}, u32[]{:S(2)}, u32[]{:S(2)}) collective-permute-start(bf16[8,2,64,128]{3,2,1,0:T(8,128)(2,1)S(1)} %collective-permute-done.5.refs_6_), channel_id=1, source_target_pairs={{0,1},{1,0},{16,17},{17,16},{32,33},{33,32},{48,49},{49,48},{64,65... | collective-permute-start | bytes 786440 | tf_op jit(solution)/shard_map/ppermute | solution.py:250
  63.6 0.0 collective-permute-done.2.refs_3_
  63.6 0.1 collective-permute-start.8
  63.7 0.0 collective-permute-done.4.refs_5_
  63.7 0.4 collective-permute-start.10
  64.1 0.0 collective-permute-done.11.refs_12_
  64.1 2.3 %collective-permute-start.12 = (bf16[8,2,64,128]{3,2,1,0:T(8,128)(2,1)S(1)}, bf16[8,2,64,128]{3,2,1,0:T(8,128)(2,1)S(1)}, u32[]{:S(2)}, u32[]{:S(2)}) collective-permute-start(bf16[8,2,64,128]{3,2,1,0:T(8,128)(2,1)S(1)} %collective-permute-done.11.refs_12_), channel_id=1, source_target_pairs={{0,1},{1,0},{16,17},{17,16},{32,33},{33,32},{48,49},{49,48},{64,65... | collective-permute-start | bytes 786440 | tf_op jit(solution)/shard_map/ppermute | solution.py:250
  66.4 0.0 collective-permute-done.13.refs_14_
  66.4 4.8 %collective-permute-start.14 = (bf16[8,2,64,128]{3,2,1,0:T(8,128)(2,1)S(1)}, bf16[8,2,64,128]{3,2,1,0:T(8,128)(2,1)}, u32[]{:S(2)}, u32[]{:S(2)}) collective-permute-start(bf16[8,2,64,128]{3,2,1,0:T(8,128)(2,1)S(1)} %collective-permute-done.13.refs_14_), channel_id=1, source_target_pairs={{0,1},{1,0},{16,17},{17,16},{32,33},{33,32},{48,49},{49,48},{64,65... | collective-permute-start | bytes 786440 | tf_op jit(solution)/shard_map/ppermute | solution.py:250
  71.2 0.0 collective-permute-done.6.refs_7_
  71.2 0.0 collective-permute-done.8.refs_9_
  71.2 0.0 copy-start.14
  71.2 0.0 collective-permute-done.10.refs_11_
  71.2 0.0 collective-permute-done.12.refs_13_
  71.2 0.6 copy-done.13
  71.9 0.1 copy-done.14
  72.0 0.1 copy-done.15
  72.1 0.7 copy-done.16
  72.8 0.0 collective-permute-done.14.refs_15_
  72.8 0.0 all-to-all-done.q_ref
  72.8 0.0 copy-done.3
  72.8 0.0 copy-done.4
  72.8 0.0 copy-done.5
  72.9 17.3 %shard_map.47 = bf16[8,64,1024]{2,1,0:T(8,128)(2,1)S(1)} custom-call(s32[16]{0:T(128)S(1)} %copy-done, bf16[8,64,1024]{2,1,0:T(8,128)(2,1)S(1)} %all-to-all-done.q_ref, bf16[8,2,64,128]{3,2,1,0:T(8,128)(2,1)} %copy-done.1, bf16[8,2,64,128]{3,2,1,0:T(8,128)(2,1)} %copy-done.3, bf16[8,2,64,128]{3,2,1,0:T(8,128)(2,1)} %copy-done.4, ...), custom_call_target="tpu_custom_call" | custom-call | tf_op jit(solution)/shard_map/pallas_call | solution.py:173
  90.2 33.5 %all_to_all.15.a_ref = bf16[8,64,1024]{2,1,0:T(8,128)(2,1)S(1)} all-to-all(bf16[8,64,1024]{2,1,0:T(8,128)(2,1)S(1)} %shard_map.47), channel_id=1, replica_groups=mesh['parts'=2,'uly'=8,'y'=8,'core'=2] {'y'}, dimensions={0} | all-to-all | bytes 2097152 | tf_op jit(solution)/shard_map/all_to_all | solution.py:262
  123.6 1.0 shard_map.48
  (26 shorter events, 0.0 us)
Async XLA Ops:
  0.0 15.5 %copy-start.2 = (bf16[1,64,8192]{2,1,0:T(8,128)(2,1)S(1)}, bf16[1,64,8192]{2,1,0:T(8,128)(2,1)}, u32[]{:S(2)}) copy-start(bf16[1,64,8192]{2,1,0:T(8,128)(2,1)} %param.4) | copy-start | bytes 3145732
  1.8 23.0 %all-to-all-start.1 = ((bf16[8,2,64,128]{3,2,1,0:T(8,128)(2,1)}), bf16[8,2,64,128]{3,2,1,0:T(8,128)(2,1)S(1)}, u32[]{:S(2)}, u32[]{:S(2)}) async-start(bf16[8,2,64,128]{3,2,1,0:T(8,128)(2,1)} %shard_map.46), calls=%async_computation.1 | async-start | bytes 524288 | tf_op jit(solution)/shard_map/all_to_all | solution.py:242
  24.8 15.8 %copy-start.1 = (bf16[8,2,64,128]{3,2,1,0:T(8,128)(2,1)}, bf16[8,2,64,128]{3,2,1,0:T(8,128)(2,1)S(1)}, u32[]{:S(2)}) copy-start(bf16[8,2,64,128]{3,2,1,0:T(8,128)(2,1)S(1)} %all-to-all-done.1.refs_0_) | copy-start | bytes 786436
  24.8 48.1 %copy-start = (s32[16]{0:T(128)S(1)}, s32[16]{0:T(128)}, u32[]{:S(2)}) copy-start(s32[16]{0:T(128)} %doc.1) | copy-start | bytes 196
  24.8 48.0 %all-to-all-start = ((bf16[8,64,1024]{2,1,0:T(8,128)(2,1)}), bf16[8,64,1024]{2,1,0:T(8,128)(2,1)S(1)}, u32[]{:S(2)}, u32[]{:S(2)}) async-start(bf16[8,64,1024]{2,1,0:T(8,128)(2,1)} %bitcast.5), calls=%async_computation | async-start | bytes 2097152 | tf_op jit(solution)/shard_map/all_to_all | solution.py:244
  28.7 13.1 %collective-permute-start = (bf16[8,2,64,128]{3,2,1,0:T(8,128)(2,1)S(1)}, bf16[8,2,64,128]{3,2,1,0:T(8,128)(2,1)S(1)}, u32[]{:S(2)}, u32[]{:S(2)}) collective-permute-start(bf16[8,2,64,128]{3,2,1,0:T(8,128)(2,1)S(1)} %all-to-all-done.1.refs_0_), channel_id=1, source_target_pairs={{0,1},{1,0},{16,17},{17,16},{32,33},{33,32},{48,49},{49,48},{64,65... | collective-permute-start | bytes 786440 | tf_op jit(solution)/shard_map/ppermute | solution.py:250
  40.7 5.5 %collective-permute-start.1 = (bf16[8,2,64,128]{3,2,1,0:T(8,128)(2,1)S(1)}, bf16[8,2,64,128]{3,2,1,0:T(8,128)(2,1)S(1)}, u32[]{:S(2)}, u32[]{:S(2)}) collective-permute-start(bf16[8,2,64,128]{3,2,1,0:T(8,128)(2,1)S(1)} %all-to-all-done.1.refs_0_), channel_id=1, source_target_pairs={{0,16},{1,113},{16,32},{17,1},{32,48},{33,17},{48,64},{49,33},{64,... | collective-permute-start | bytes 786440 | tf_op jit(solution)/shard_map/ppermute | solution.py:247
  41.8 31.0 %copy-start.3 = (bf16[8,2,64,128]{3,2,1,0:T(8,128)(2,1)}, bf16[8,2,64,128]{3,2,1,0:T(8,128)(2,1)S(1)}, u32[]{:S(2)}) copy-start(bf16[8,2,64,128]{3,2,1,0:T(8,128)(2,1)S(1)} %collective-permute-done.refs_1_) | copy-start | bytes 786436
  41.8 7.2 %collective-permute-start.3 = (bf16[8,2,64,128]{3,2,1,0:T(8,128)(2,1)S(1)}, bf16[8,2,64,128]{3,2,1,0:T(8,128)(2,1)S(1)}, u32[]{:S(2)}, u32[]{:S(2)}) collective-permute-start(bf16[8,2,64,128]{3,2,1,0:T(8,128)(2,1)S(1)} %collective-permute-done.refs_1_), channel_id=1, source_target_pairs={{0,16},{1,113},{16,32},{17,1},{32,48},{33,17},{48,64},{49,33},{64,... | collective-permute-start | bytes 786440 | tf_op jit(solution)/shard_map/ppermute | solution.py:247
  46.2 26.6 %copy-start.4 = (bf16[8,2,64,128]{3,2,1,0:T(8,128)(2,1)}, bf16[8,2,64,128]{3,2,1,0:T(8,128)(2,1)S(1)}, u32[]{:S(2)}) copy-start(bf16[8,2,64,128]{3,2,1,0:T(8,128)(2,1)S(1)} %collective-permute-done.1.refs_2_) | copy-start | bytes 786436
  46.2 5.6 %collective-permute-start.5 = (bf16[8,2,64,128]{3,2,1,0:T(8,128)(2,1)S(1)}, bf16[8,2,64,128]{3,2,1,0:T(8,128)(2,1)S(1)}, u32[]{:S(2)}, u32[]{:S(2)}) collective-permute-start(bf16[8,2,64,128]{3,2,1,0:T(8,128)(2,1)S(1)} %collective-permute-done.1.refs_2_), channel_id=1, source_target_pairs={{0,16},{1,113},{16,32},{17,1},{32,48},{33,17},{48,64},{49,33},{64,... | collective-permute-start | bytes 786440 | tf_op jit(solution)/shard_map/ppermute | solution.py:247
  49.0 23.8 %copy-start.5 = (bf16[8,2,64,128]{3,2,1,0:T(8,128)(2,1)}, bf16[8,2,64,128]{3,2,1,0:T(8,128)(2,1)S(1)}, u32[]{:S(2)}) copy-start(bf16[8,2,64,128]{3,2,1,0:T(8,128)(2,1)S(1)} %collective-permute-done.3.refs_4_) | copy-start | bytes 786436
  49.0 7.1 %collective-permute-start.7 = (bf16[8,2,64,128]{3,2,1,0:T(8,128)(2,1)S(1)}, bf16[8,2,64,128]{3,2,1,0:T(8,128)(2,1)S(1)}, u32[]{:S(2)}, u32[]{:S(2)}) collective-permute-start(bf16[8,2,64,128]{3,2,1,0:T(8,128)(2,1)S(1)} %collective-permute-done.3.refs_4_), channel_id=1, source_target_pairs={{0,16},{1,113},{16,32},{17,1},{32,48},{33,17},{48,64},{49,33},{64,... | collective-permute-start | bytes 786440 | tf_op jit(solution)/shard_map/ppermute | solution.py:247
  51.8 21.0 %copy-start.6 = (bf16[8,2,64,128]{3,2,1,0:T(8,128)(2,1)}, bf16[8,2,64,128]{3,2,1,0:T(8,128)(2,1)S(1)}, u32[]{:S(2)}) copy-start(bf16[8,2,64,128]{3,2,1,0:T(8,128)(2,1)S(1)} %collective-permute-done.5.refs_6_) | copy-start | bytes 786436
  51.8 7.3 %collective-permute-start.9 = (bf16[8,2,64,128]{3,2,1,0:T(8,128)(2,1)S(1)}, bf16[8,2,64,128]{3,2,1,0:T(8,128)(2,1)S(1)}, u32[]{:S(2)}, u32[]{:S(2)}) collective-permute-start(bf16[8,2,64,128]{3,2,1,0:T(8,128)(2,1)S(1)} %collective-permute-done.5.refs_6_), channel_id=1, source_target_pairs={{0,16},{1,113},{16,32},{17,1},{32,48},{33,17},{48,64},{49,33},{64,... | collective-permute-start | bytes 786440 | tf_op jit(solution)/shard_map/ppermute | solution.py:247
  54.1 9.4 %collective-permute-start.2 = (bf16[8,2,64,128]{3,2,1,0:T(8,128)(2,1)S(1)}, bf16[8,2,64,128]{3,2,1,0:T(8,128)(2,1)S(1)}, u32[]{:S(2)}, u32[]{:S(2)}) collective-permute-start(bf16[8,2,64,128]{3,2,1,0:T(8,128)(2,1)S(1)} %collective-permute-done.1.refs_2_), channel_id=1, source_target_pairs={{0,1},{1,0},{16,17},{17,16},{32,33},{33,32},{48,49},{49,48},{64,65... | collective-permute-start | bytes 786440 | tf_op jit(solution)/shard_map/ppermute | solution.py:250
  56.0 7.7 %collective-permute-start.4 = (bf16[8,2,64,128]{3,2,1,0:T(8,128)(2,1)S(1)}, bf16[8,2,64,128]{3,2,1,0:T(8,128)(2,1)S(1)}, u32[]{:S(2)}, u32[]{:S(2)}) collective-permute-start(bf16[8,2,64,128]{3,2,1,0:T(8,128)(2,1)S(1)} %collective-permute-done.3.refs_4_), channel_id=1, source_target_pairs={{0,1},{1,0},{16,17},{17,16},{32,33},{33,32},{48,49},{49,48},{64,65... | collective-permute-start | bytes 786440 | tf_op jit(solution)/shard_map/ppermute | solution.py:250
  56.1 16.7 %copy-start.7 = (bf16[8,2,64,128]{3,2,1,0:T(8,128)(2,1)}, bf16[8,2,64,128]{3,2,1,0:T(8,128)(2,1)S(1)}, u32[]{:S(2)}) copy-start(bf16[8,2,64,128]{3,2,1,0:T(8,128)(2,1)S(1)} %collective-permute-done.7.refs_8_) | copy-start | bytes 786436
  56.1 8.0 %collective-permute-start.11 = (bf16[8,2,64,128]{3,2,1,0:T(8,128)(2,1)S(1)}, bf16[8,2,64,128]{3,2,1,0:T(8,128)(2,1)S(1)}, u32[]{:S(2)}, u32[]{:S(2)}) collective-permute-start(bf16[8,2,64,128]{3,2,1,0:T(8,128)(2,1)S(1)} %collective-permute-done.7.refs_8_), channel_id=1, source_target_pairs={{0,16},{1,113},{16,32},{17,1},{32,48},{33,17},{48,64},{49,33},{64,... | collective-permute-start | bytes 786440 | tf_op jit(solution)/shard_map/ppermute | solution.py:247
  59.1 13.8 %copy-start.8 = (bf16[8,2,64,128]{3,2,1,0:T(8,128)(2,1)}, bf16[8,2,64,128]{3,2,1,0:T(8,128)(2,1)S(1)}, u32[]{:S(2)}) copy-start(bf16[8,2,64,128]{3,2,1,0:T(8,128)(2,1)S(1)} %collective-permute-done.9.refs_10_) | copy-start | bytes 786436
  59.1 7.3 %collective-permute-start.13 = (bf16[8,2,64,128]{3,2,1,0:T(8,128)(2,1)S(1)}, bf16[8,2,64,128]{3,2,1,0:T(8,128)(2,1)S(1)}, u32[]{:S(2)}, u32[]{:S(2)}) collective-permute-start(bf16[8,2,64,128]{3,2,1,0:T(8,128)(2,1)S(1)} %collective-permute-done.9.refs_10_), channel_id=1, source_target_pairs={{0,16},{1,113},{16,32},{17,1},{32,48},{33,17},{48,64},{49,33},{64,... | collective-permute-start | bytes 786440 | tf_op jit(solution)/shard_map/ppermute | solution.py:247
  60.9 10.3 %collective-permute-start.6 = (bf16[8,2,64,128]{3,2,1,0:T(8,128)(2,1)S(1)}, bf16[8,2,64,128]{3,2,1,0:T(8,128)(2,1)S(1)}, u32[]{:S(2)}, u32[]{:S(2)}) collective-permute-start(bf16[8,2,64,128]{3,2,1,0:T(8,128)(2,1)S(1)} %collective-permute-done.5.refs_6_), channel_id=1, source_target_pairs={{0,1},{1,0},{16,17},{17,16},{32,33},{33,32},{48,49},{49,48},{64,65... | collective-permute-start | bytes 786440 | tf_op jit(solution)/shard_map/ppermute | solution.py:250
  63.6 9.3 %copy-start.9 = (bf16[8,2,64,128]{3,2,1,0:T(8,128)(2,1)}, bf16[8,2,64,128]{3,2,1,0:T(8,128)(2,1)S(1)}, u32[]{:S(2)}) copy-start(bf16[8,2,64,128]{3,2,1,0:T(8,128)(2,1)S(1)} %collective-permute-done.2.refs_3_) | copy-start | bytes 786436
  63.6 7.6 %collective-permute-start.8 = (bf16[8,2,64,128]{3,2,1,0:T(8,128)(2,1)S(1)}, bf16[8,2,64,128]{3,2,1,0:T(8,128)(2,1)S(1)}, u32[]{:S(2)}, u32[]{:S(2)}) collective-permute-start(bf16[8,2,64,128]{3,2,1,0:T(8,128)(2,1)S(1)} %collective-permute-done.7.refs_8_), channel_id=1, source_target_pairs={{0,1},{1,0},{16,17},{17,16},{32,33},{33,32},{48,49},{49,48},{64,65... | collective-permute-start | bytes 786440 | tf_op jit(solution)/shard_map/ppermute | solution.py:250
  63.7 9.1 %copy-start.10 = (bf16[8,2,64,128]{3,2,1,0:T(8,128)(2,1)}, bf16[8,2,64,128]{3,2,1,0:T(8,128)(2,1)S(1)}, u32[]{:S(2)}) copy-start(bf16[8,2,64,128]{3,2,1,0:T(8,128)(2,1)S(1)} %collective-permute-done.4.refs_5_) | copy-start | bytes 786436
  63.7 7.5 %collective-permute-start.10 = (bf16[8,2,64,128]{3,2,1,0:T(8,128)(2,1)S(1)}, bf16[8,2,64,128]{3,2,1,0:T(8,128)(2,1)S(1)}, u32[]{:S(2)}, u32[]{:S(2)}) collective-permute-start(bf16[8,2,64,128]{3,2,1,0:T(8,128)(2,1)S(1)} %collective-permute-done.9.refs_10_), channel_id=1, source_target_pairs={{0,1},{1,0},{16,17},{17,16},{32,33},{33,32},{48,49},{49,48},{64,65... | collective-permute-start | bytes 786440 | tf_op jit(solution)/shard_map/ppermute | solution.py:250
  64.1 8.8 %copy-start.11 = (bf16[8,2,64,128]{3,2,1,0:T(8,128)(2,1)}, bf16[8,2,64,128]{3,2,1,0:T(8,128)(2,1)S(1)}, u32[]{:S(2)}) copy-start(bf16[8,2,64,128]{3,2,1,0:T(8,128)(2,1)S(1)} %collective-permute-done.11.refs_12_) | copy-start | bytes 786436
  64.1 7.1 %collective-permute-start.12 = (bf16[8,2,64,128]{3,2,1,0:T(8,128)(2,1)S(1)}, bf16[8,2,64,128]{3,2,1,0:T(8,128)(2,1)S(1)}, u32[]{:S(2)}, u32[]{:S(2)}) collective-permute-start(bf16[8,2,64,128]{3,2,1,0:T(8,128)(2,1)S(1)} %collective-permute-done.11.refs_12_), channel_id=1, source_target_pairs={{0,1},{1,0},{16,17},{17,16},{32,33},{33,32},{48,49},{49,48},{64,65... | collective-permute-start | bytes 786440 | tf_op jit(solution)/shard_map/ppermute | solution.py:250
  66.4 4.8 %copy-start.12 = (bf16[8,2,64,128]{3,2,1,0:T(8,128)(2,1)}, bf16[8,2,64,128]{3,2,1,0:T(8,128)(2,1)S(1)}, u32[]{:S(2)}) copy-start(bf16[8,2,64,128]{3,2,1,0:T(8,128)(2,1)S(1)} %collective-permute-done.13.refs_14_) | copy-start | bytes 786436
  66.4 6.4 %collective-permute-start.14 = (bf16[8,2,64,128]{3,2,1,0:T(8,128)(2,1)S(1)}, bf16[8,2,64,128]{3,2,1,0:T(8,128)(2,1)}, u32[]{:S(2)}, u32[]{:S(2)}) collective-permute-start(bf16[8,2,64,128]{3,2,1,0:T(8,128)(2,1)S(1)} %collective-permute-done.13.refs_14_), channel_id=1, source_target_pairs={{0,1},{1,0},{16,17},{17,16},{32,33},{33,32},{48,49},{49,48},{64,65... | collective-permute-start | bytes 786440 | tf_op jit(solution)/shard_map/ppermute | solution.py:250
  71.2 0.7 copy-start.13
  71.2 0.8 copy-start.14
  71.2 0.9 copy-start.15
  72.1 0.7 copy-start.16
